TPU v7x, 256 devices: a whole 4x4x8 slice. The times are simulated.
256 devices in a mesh: col: 32 (over z, y), row: 8 (over x, core).
Axes of the slice: x: 4, y: 4, z: 8, core: 2. Of those that a mesh axis runs over, the one named last changes fastest.
Arguments:
- inter_mask: int32 [65536, 4096], P('row', 'col')
- emb_user: bfloat16 [65536, 64], P(('row', 'col'))
- emb_item: bfloat16 [4096, 64], P(('col', 'row'))
- triples: int32 [128, 3], replicated
Outputs:
- output 1: bfloat16 [65536, 64], P(('row', 'col'))
- output 2: bfloat16 [4096, 64], P(('col', 'row'))
- output 3: float32 [], replicated
All inputs are finite; a program needn't handle non-finite values.
Results may differ from a plain program's by a relative error of at most 0.00519882.
Values are sent between devices in bfloat16 or wider.
A program may use at most 768 MiB of HBM per device.

v0:
```python
import jax
import jax.numpy as jnp
from jax import lax
from jax.sharding import PartitionSpec as P, NamedSharding

LAYERS = 3


def lookup_rows(emb_table, row_ids, row_base):
    local_ids = row_ids - row_base
    inside = (local_ids >= 0) & (local_ids < emb_table.shape[0])
    got_rows = jnp.take(emb_table, jnp.clip(local_ids, 0, emb_table.shape[0] - 1), axis=0).astype(jnp.float32)
    return jnp.where(inside[:, None], got_rows, 0.0)


def solution(mesh):
    row_count = mesh.shape["row"]
    col_count = mesh.shape["col"]

    def local_prog(mask_blk, user_shard, item_shard, triples):
        row_idx = lax.axis_index("row")
        col_idx = lax.axis_index("col")
        deg_user = jnp.maximum(lax.psum(jnp.sum(mask_blk, axis=1), "col"), 1)
        deg_item = jnp.maximum(lax.psum(jnp.sum(mask_blk, axis=0), "row"), 1)
        scale_user = lax.rsqrt(deg_user.astype(jnp.float32))
        scale_item = lax.rsqrt(deg_item.astype(jnp.float32))
        norm_adj = (mask_blk.astype(jnp.float32) * scale_user[:, None] * scale_item[None, :]).astype(jnp.bfloat16)
        layer_user = user_shard
        layer_item = item_shard
        total_user = user_shard.astype(jnp.float32)
        total_item = item_shard.astype(jnp.float32)
        for layer_idx in range(LAYERS):
            item_panel = lax.all_gather(layer_item, "row", axis=0, tiled=True)
            user_part = jnp.dot(norm_adj, item_panel, preferred_element_type=jnp.float32)
            next_user = lax.psum_scatter(user_part, "col", scatter_dimension=0, tiled=True).astype(jnp.bfloat16)
            user_panel = lax.all_gather(layer_user, "col", axis=0, tiled=True)
            item_part = lax.dot_general(norm_adj, user_panel, (((0,), (0,)), ((), ())), preferred_element_type=jnp.float32)
            next_item = lax.psum_scatter(item_part, "row", scatter_dimension=0, tiled=True).astype(jnp.bfloat16)
            total_user = total_user + next_user.astype(jnp.float32)
            total_item = total_item + next_item.astype(jnp.float32)
            layer_user = next_user
            layer_item = next_item
        out_user = (total_user / (LAYERS + 1)).astype(jnp.bfloat16)
        out_item = (total_item / (LAYERS + 1)).astype(jnp.bfloat16)
        user_base = (row_idx * col_count + col_idx) * out_user.shape[0]
        item_base = (col_idx * row_count + row_idx) * out_item.shape[0]
        trip_count = triples.shape[0]
        picked = jnp.concatenate([lookup_rows(out_user, triples[:, 0], user_base), lookup_rows(out_item, triples[:, 1], item_base), lookup_rows(out_item, triples[:, 2], item_base)], axis=0)
        picked = lax.psum(picked, ("row", "col"))
        user_vec = picked[:trip_count]
        pos_vec = picked[trip_count:2 * trip_count]
        neg_vec = picked[2 * trip_count:]
        margin = jnp.sum(user_vec * pos_vec, axis=1) - jnp.sum(user_vec * neg_vec, axis=1)
        bpr_loss = jnp.mean(jax.nn.softplus(-margin))
        return out_user, out_item, bpr_loss

    return jax.shard_map(local_prog, mesh=mesh, in_specs=(P("row", "col"), P(("row", "col"), None), P(("col", "row"), None), P(None, None)), out_specs=(P(("row", "col"), None), P(("col", "row"), None), P()), check_vma=False)
```

profile of v0, /device:TPU:1, one launch (start us, length us, event | category | flops | bytes accessed | tf_op | source)
XLA Modules:
  0.0 1376.2 jit_solution(743145191135464015)
XLA Ops:
  8.0 3.3 fusion.3
  11.3 8.5 psum.22
  19.8 118.8 %psum.21 = s32[8192]{0:T(1024)S(1)} all-reduce(s32[8192]{0:T(1024)S(1)} %get-tuple-element.4), channel_id=1, replica_groups=mesh['col'=32,'row'=8] {'col'}, use_global_device_ids=true, to_apply=%region_1.0 | all-reduce | flops 8192 | bytes 65536 | tf_op jit(solution)/shard_map/psum | solution.py:23
  138.7 42.0 %all_gather.18 = bf16[128,64]{1,0:T(8,128)(2,1)S(1)} all-gather(bf16[16,64]{1,0:T(8,128)(2,1)S(1)} %copy-done.6), channel_id=1, replica_groups=mesh['col'=32,'row'=8] {'row'}, dimensions={0}, use_global_device_ids=true | all-gather | bytes 18432 | tf_op jit(solution)/shard_map/all_gather | solution.py:33
  180.7 2.9 multiply_convert_fusion
  183.6 2.6 fusion.5
  186.2 2.2 fusion.4
  188.5 21.5 %reduce-scatter.9.cloned.1.call-done = f32[16,64]{1,0:T(8,128)} async-done(((f32[128,64]{1,0:T(8,128)}), f32[16,64]{1,0:T(8,128)}) %reduce-scatter.9.cloned.1.call-update) | async-done | bytes 4112 | tf_op jit(solution)/shard_map/reduce_scatter | solution.py:38
  210.0 0.7 convert_element_type.76
  210.7 15.3 %all_gather.20 = bf16[128,64]{1,0:T(8,128)(2,1)S(1)} all-gather(bf16[16,64]{1,0:T(8,128)(2,1)S(1)} %convert_element_type.76), channel_id=1, replica_groups=mesh['col'=32,'row'=8] {'row'}, dimensions={0}, use_global_device_ids=true | all-gather | bytes 18432 | tf_op jit(solution)/shard_map/all_gather | solution.py:33
  226.0 2.2 fusion.6
  228.3 199.8 %reduce-scatter.7.cloned.1.call-done = f32[256,64]{0,1:T(8,128)} async-done(((f32[8192,64]{0,1:T(8,128)}), f32[256,64]{0,1:T(8,128)}) %reduce-scatter.7.cloned.1.call-update) | async-done | bytes 65552 | tf_op jit(solution)/shard_map/reduce_scatter | solution.py:35
  428.1 1.5 convert_element_type.74
  429.6 219.0 %reduce-scatter.11.cloned.1.call-done = f32[256,64]{0,1:T(8,128)} async-done(((f32[8192,64]{0,1:T(8,128)}), f32[256,64]{0,1:T(8,128)}) %reduce-scatter.11.cloned.1.call-update) | async-done | bytes 65552 | tf_op jit(solution)/shard_map/reduce_scatter | solution.py:35
  648.6 1.5 convert_element_type.77
  650.2 70.5 %all-gather.6.cloned.1.call-done = bf16[8192,64]{0,1:T(8,128)(2,1)} async-done(((bf16[256,64]{0,1:T(8,128)(2,1)}), bf16[8192,64]{0,1:T(8,128)(2,1)}) %all-gather.6.cloned.1.call-update) | async-done | bytes 1048592 | tf_op jit(solution)/shard_map/all_gather | solution.py:36
  720.7 2.6 fusion.7
  723.3 69.9 %all-gather.8.cloned.1.call-done = bf16[8192,64]{0,1:T(8,128)(2,1)} async-done(((bf16[256,64]{0,1:T(8,128)(2,1)}), bf16[8192,64]{0,1:T(8,128)(2,1)}) %all-gather.8.cloned.1.call-update) | async-done | bytes 1048592 | tf_op jit(solution)/shard_map/all_gather | solution.py:36
  793.3 2.6 fusion.9
  795.9 34.4 %reduce-scatter.13.cloned.1.call-done = f32[16,64]{1,0:T(8,128)} async-done(((f32[128,64]{1,0:T(8,128)}), f32[16,64]{1,0:T(8,128)}) %reduce-scatter.13.cloned.1.call-update) | async-done | bytes 4112 | tf_op jit(solution)/shard_map/reduce_scatter | solution.py:38
  830.4 34.5 %reduce-scatter.17.cloned.1.call-done = f32[16,64]{1,0:T(8,128)} async-done(((f32[128,64]{1,0:T(8,128)}), f32[16,64]{1,0:T(8,128)}) %reduce-scatter.17.cloned.1.call-update) | async-done | bytes 4112 | tf_op jit(solution)/shard_map/reduce_scatter | solution.py:38
  864.9 0.7 multiply_convert_fusion.2
  865.6 15.4 %all_gather.22 = bf16[128,64]{1,0:T(8,128)(2,1)S(1)} all-gather(bf16[16,64]{1,0:T(8,128)(2,1)S(1)} %get-tuple-element.15), channel_id=1, replica_groups=mesh['col'=32,'row'=8] {'row'}, dimensions={0}, use_global_device_ids=true | all-gather | bytes 18432 | tf_op jit(solution)/shard_map/all_gather | solution.py:33
  881.0 2.2 fusion.8
  883.9 0.7 gather_fusion.2
  884.7 0.7 gather_fusion.1
  885.5 210.1 %reduce-scatter.15.cloned.1.call-done = f32[256,64]{0,1:T(8,128)} async-done(((f32[8192,64]{0,1:T(8,128)}), f32[256,64]{0,1:T(8,128)}) %reduce-scatter.15.cloned.1.call-update) | async-done | bytes 65552 | tf_op jit(solution)/shard_map/reduce_scatter | solution.py:35
  1095.7 0.9 multiply_convert_fusion.1
  1096.6 0.7 gather_fusion
  1097.5 0.7 pad_maximum_fusion
  1098.2 267.8 %all-reduce.2.cloned.1.call-done = f32[384,64]{1,0:T(8,128)} async-done(((f32[384,64]{1,0:T(8,128)}), f32[384,64]{1,0:T(8,128)}) %all-reduce.2.cloned.1.call-update) | async-done | bytes 98320 | tf_op jit(solution)/shard_map/psum | solution.py:49
  1366.0 1.0 fusion
  (48 shorter events, 2.9 us)
Async XLA Ops:
  7.2 176.4 %all-gather.4.cloned.1.call-start = ((), (), s32[]{:S(2)}) async-start(), calls=%async_computation.7 | async-start | bytes 1081344 | tf_op jit(solution)/shard_map/all_gather | solution.py:36
  7.9 130.8 %copy-start.6 = (bf16[16,64]{1,0:T(8,128)(2,1)S(1)}, bf16[16,64]{1,0:T(8,128)(2,1)}, u32[]{:S(2)}) copy-start(bf16[16,64]{1,0:T(8,128)(2,1)} %param.8) | copy-start | bytes 6148
  7.9 202.1 %reduce-scatter.9.cloned.1.call-start = ((), (), s32[]{:S(2)}) async-start(), calls=%async_computation.8 | async-start | bytes 73728 | tf_op jit(solution)/shard_map/reduce_scatter | solution.py:38
  186.2 241.9 %reduce-scatter.7.cloned.1.call-start = ((), (), s32[]{:S(2)}) async-start(), calls=%async_computation.6 | async-start | bytes 2162688 | tf_op jit(solution)/shard_map/reduce_scatter | solution.py:35
  188.4 460.2 %reduce-scatter.11.cloned.1.call-start = ((), (), s32[]{:S(2)}) async-start(), calls=%async_computation.9 | async-start | bytes 2162688 | tf_op jit(solution)/shard_map/reduce_scatter | solution.py:35
  228.2 492.4 %all-gather.6.cloned.1.call-start = ((), (), s32[]{:S(2)}) async-start(), calls=%async_computation.10 | async-start | bytes 1081344 | tf_op jit(solution)/shard_map/all_gather | solution.py:36
  429.5 363.7 %all-gather.8.cloned.1.call-start = ((), (), s32[]{:S(2)}) async-start(), calls=%async_computation.13 | async-start | bytes 1081344 | tf_op jit(solution)/shard_map/all_gather | solution.py:36
  650.1 180.2 %reduce-scatter.13.cloned.1.call-start = ((), (), s32[]{:S(2)}) async-start(), calls=%async_computation.11 | async-start | bytes 73728 | tf_op jit(solution)/shard_map/reduce_scatter | solution.py:38
  723.3 141.6 %copy-start.5 = (f32[16,64]{1,0:T(8,128)S(1)}, f32[16,64]{1,0:T(8,128)}, u32[]{:S(2)}) copy-start(f32[16,64]{1,0:T(8,128)} %reduce-scatter.9.cloned.1.call-done) | copy-start | bytes 12292
  723.3 141.6 %reduce-scatter.17.cloned.1.call-start = ((), (), s32[]{:S(2)}) async-start(), calls=%async_computation.14 | async-start | bytes 73728 | tf_op jit(solution)/shard_map/reduce_scatter | solution.py:38
  795.9 299.8 %reduce-scatter.15.cloned.1.call-start = ((), (), s32[]{:S(2)}) async-start(), calls=%async_computation.12 | async-start | bytes 2162688 | tf_op jit(solution)/shard_map/reduce_scatter | solution.py:35
  865.6 19.1 %copy-start = (bf16[16,64]{1,0:T(8,128)(2,1)}, bf16[16,64]{1,0:T(8,128)(2,1)S(1)}, u32[]{:S(2)}) copy-start(bf16[16,64]{1,0:T(8,128)(2,1)S(1)} %get-tuple-element.14) | copy-start | bytes 6148
  883.2 0.7 copy-start.7
  883.2 212.5 %copy-start.1 = (f32[256,64]{0,1:T(8,128)S(1)}, f32[256,64]{0,1:T(8,128)}, u32[]{:S(2)}) copy-start(f32[256,64]{0,1:T(8,128)} %reduce-scatter.7.cloned.1.call-done) | copy-start | bytes 196612
  883.2 212.5 %copy-start.2 = (f32[256,64]{0,1:T(8,128)S(1)}, f32[256,64]{0,1:T(8,128)}, u32[]{:S(2)}) copy-start(f32[256,64]{0,1:T(8,128)} %reduce-scatter.11.cloned.1.call-done) | copy-start | bytes 196612
  883.2 212.5 %copy-start.4 = (bf16[256,64]{0,1:T(8,128)(2,1)S(1)}, bf16[256,64]{0,1:T(8,128)(2,1)}, u32[]{:S(2)}) copy-start(bf16[256,64]{0,1:T(8,128)(2,1)} %param.7) | copy-start | bytes 98308
  883.2 482.7 %all-reduce.2.cloned.1.call-start = ((), (), s32[]{:S(2)}) async-start(), calls=%async_computation.15 | async-start | bytes 393216 | tf_op jit(solution)/shard_map/psum | solution.py:49
  1096.5 271.7 %copy-start.3 = (bf16[256,64]{0,1:T(8,128)(2,1)}, bf16[256,64]{0,1:T(8,128)(2,1)S(1)}, u32[]{:S(2)}) copy-start(bf16[256,64]{0,1:T(8,128)(2,1)S(1)} %multiply_convert_fusion.1) | copy-start | bytes 98308
Sparse Core Ops, SparseCore 0:
  10.4 69.7 all-gather.3
  186.3 23.6 reduce-scatter.8
  213.8 214.1 reduce-scatter.6
  431.7 216.8 reduce-scatter.10
  650.9 69.6 all-gather.5
  723.6 69.6 all-gather.7
  795.7 34.5 reduce-scatter.12
  832.8 31.9 reduce-scatter.16
  883.3 212.2 reduce-scatter.14
  1101.0 264.9 all-reduce.1
where the time goes:
time: 1380 us
  waiting for transfers between devices  1130 us (82%)
  blocking collectives  200 us (14%)
  between operations  16.1 us (1%)
  matrix products  14.4 us (1%)
  other arithmetic  14 us (1%)
    reduce_scatter x3, waiting for transfers between devices, local_prog(): lax.psum_scatter(user_part, 'col', scatter_dimension=0, tiled=True)  629 us
    psum x1, waiting for transfers between devices, local_prog(): picked = lax.psum(picked, ('row', 'col'))  268 us
    all_gather x3, waiting for transfers between devices, local_prog(): user_panel = lax.all_gather(layer_user, 'col', axis=0, tiled=True)  140 us
    psum x1, blocking collectives, local_prog(): deg_user = jnp.maximum(lax.psum(jnp.sum(mask_blk, axis=1), 'col'), 1)  119 us
    reduce_scatter x3, waiting for transfers between devices, local_prog(): lax.psum_scatter(item_part, 'row', scatter_dimension=0, tiled=True)  90.4 us
    all_gather x3, blocking collectives, local_prog(): item_panel = lax.all_gather(layer_item, 'row', axis=0, tiled=True)  72.6 us
  transfers between devices with their start and end apart: 10, of which 9 were waited for; matrix products, arithmetic and copies ran while one was open for 2% of the time, Pallas kernels for 0%

commit v1 on v0

v1 whole, which is shorter than its diff:
```python
import functools

import jax
import jax.numpy as jnp
from jax import lax
from jax.experimental import pallas as pl
from jax.experimental.pallas import tpu as pltpu
from jax.sharding import PartitionSpec as P

MESH = pl.DeviceIdType.MESH
F32 = jnp.float32
BF16 = jnp.bfloat16
FEAT = 64
TRIPLES = 128
LAYERS = 3


def kernel(dims, mask, eu0, ei0, trip, out_user, out_item, loss, *scratch):
    Z, Y, X, SH, UD = dims
    C, R, Q = Z * Y, 2 * X, Y * X
    IB = R * SH
    HS = SH // 2
    (deg_s, deg_r, deg_f, own_deg, ideg, send_a, slab, slab_t, tbl0, tbl_j, acc, eu_j, eu_2, p_j, rd_j, s1_j, rxy_j, s2_j, rz_j,
     p_3, rd_3, s1_3, rxy_3, s2_3, rz_3, pk_z, pk_q, pk_d, xc, xr, sends, recvs, a2a_recv) = scratch
    row = lax.axis_index("row")
    col = lax.axis_index("col")
    core, x = row % 2, row // 2
    z, y = col // Y, col % Y
    q = y * X + x
    mate = x * 2 + (1 - core)

    def remote(src, dst, sem, r, c, recv=None):
        return pltpu.make_async_remote_copy(
            src_ref=src, dst_ref=dst, send_sem=sends.at[sem], recv_sem=recvs.at[sem] if recv is None else recv,
            device_id=(c, r), device_id_type=MESH)

    def await_recv(ref, sem):
        remote(ref, ref, sem, row, col).wait_recv()

    def await_send(ref, sem):
        remote(ref, ref, sem, row, col).wait_send()

    def q_to_rc(p):
        return (p % X) * 2 + core, z * Y + p // X

    barrier = pltpu.get_barrier_semaphore()

    def hail_col(k, _):
        pl.semaphore_signal(barrier, inc=1, device_id=((col + k) % C, row), device_id_type=MESH)
        return 0

    def hail_row(k, _):
        pl.semaphore_signal(barrier, inc=1, device_id=(col, (row + k) % R), device_id_type=MESH)
        return 0

    def hail_diag(k, _):
        ny = (y + 1 + k // (X - 1)) % Y
        nx = (x + 1 + k % (X - 1)) % X
        pl.semaphore_signal(barrier, inc=1, device_id=(z * Y + ny, nx * 2 + core), device_id_type=MESH)
        return 0

    lax.fori_loop(1, C, hail_col, 0)
    lax.fori_loop(1, R, hail_row, 0)
    lax.fori_loop(0, (X - 1) * (Y - 1), hail_diag, 0)

    ones = jnp.ones((8, IB), BF16)

    def count(k, part):
        blk = mask[k].astype(F32)
        sums = lax.dot_general(ones, blk.astype(BF16), (((1,), (1,)), ((), ())), preferred_element_type=F32)
        deg_s[k] = sums[0:1]
        return part + jnp.sum(blk.reshape(UD // 8, 8, IB), axis=0)

    part = lax.fori_loop(0, C, count, jnp.zeros((8, IB), F32))
    ideg[row] = jnp.sum(part, axis=0, keepdims=True)
    deg_r[col] = deg_s[col]
    tbl0[core, q, z] = ei0[...]
    pl.semaphore_wait(barrier, (C - 1) + (R - 1) + (X - 1) * (Y - 1))

    def send_deg(k, _):
        to = (col + k) % C
        remote(deg_s.at[to], deg_r.at[col], 0, row, to).start()
        return 0

    def send_ideg(k, _):
        remote(ideg.at[row], ideg.at[row], 1, (row + k) % R, col).start()
        return 0

    def gather_z(tbl, sem):
        def go(k, _):
            to = (z + k) % Z
            remote(tbl.at[core, q, z], tbl.at[core, q, z], sem, row, to * Y + y).start()
            return 0
        lax.fori_loop(1, Z, go, 0)

    def gather_q(tbl, sem):
        await_recv(tbl.at[core, q, pl.ds(0, Z - 1)], sem)

        def go(k, _):
            r, c = q_to_rc((q + k) % Q)
            remote(tbl.at[core, q], tbl.at[core, q], sem + 1, r, c).start()
            return 0
        lax.fori_loop(1, Q, go, 0)

    def gather_d(tbl, sem):
        await_recv(tbl.at[core, pl.ds(0, Q - 1)], sem + 1)
        remote(tbl.at[core], tbl.at[core], sem + 2, mate, col).start()

    def gather_end(tbl, sem):
        await_recv(tbl.at[core], sem + 2)
        await_send(tbl.at[core, q, pl.ds(0, Z - 1)], sem)
        await_send(tbl.at[core, pl.ds(0, Q - 1)], sem + 1)
        await_send(tbl.at[core], sem + 2)

    lax.fori_loop(1, C, send_deg, 0)
    lax.fori_loop(1, R, send_ideg, 0)
    gather_z(tbl0, 4)
    await_recv(deg_r.at[pl.ds(0, C - 1)], 0)

    own_deg[...] = lax.fori_loop(0, C, lambda k, t: t + deg_r[k], jnp.zeros((1, UD), F32))
    deg_f[col] = own_deg[...]

    def spread_deg(k, _):
        remote(own_deg, deg_f.at[col], 2, row, (col + k) % C).start()
        return 0

    lax.fori_loop(1, C, spread_deg, 0)
    await_recv(ideg.at[pl.ds(0, R - 1)], 1)
    scale_item = lax.rsqrt(jnp.maximum(lax.fori_loop(0, R, lambda k, t: t + ideg[k], jnp.zeros((1, IB), F32)), 1.0))
    gather_q(tbl0, 4)
    await_recv(deg_f.at[pl.ds(0, C - 1)], 2)

    def order(k):
        j, dy = k // Y, (k + 1) % Y
        m = Z // 2 - (j + 1) // 2
        odd = j % 2
        dz = (odd * m + (1 - odd) * (Z - m)) % Z
        return dz, dy

    def piece(c):
        scale = lax.rsqrt(jnp.maximum(deg_f[c], 1.0))
        scale = jnp.transpose(jnp.broadcast_to(scale, (IB, UD)))
        return (mask[c].astype(F32) * scale * scale_item).astype(BF16)

    def target(k):
        dz, dy = order(k)
        return ((z + dz) % Z) * Y + (y + dy) % Y

    def ship(k):
        to = target(k)
        remote(send_a.at[to], slab.at[col], 3, row, to, recv=a2a_recv.at[col]).start()

    send_a[target(0)] = piece(target(0))

    def make_and_ship(k, _):
        send_a[target(k)] = piece(target(k))
        ship(k - 1)
        return 0

    lax.fori_loop(1, C - 1, make_and_ship, 0)
    slab[col] = piece(col)
    ship(C - 2)
    gather_d(tbl0, 4)
    gather_end(tbl0, 4)

    def rows_of(tbl, c):
        cz, cy = c // Y, c % Y
        return jnp.concatenate([tbl[i % 2, cy * X + i // 2, cz] for i in range(R)], axis=0)

    def use(c):
        blk = slab[c]
        slab_t[c] = jnp.transpose(blk)
        acc[...] += jnp.dot(blk, rows_of(tbl0, c), preferred_element_type=F32)

    acc[...] = jnp.zeros_like(acc)
    use(col)

    def arrive(k, _):
        dz, dy = order(k)
        c = ((z - dz + Z) % Z) * Y + (y - dy + Y) % Y
        pltpu.make_async_remote_copy(src_ref=slab.at[c], dst_ref=slab.at[c], send_sem=sends.at[3], recv_sem=a2a_recv.at[c],
                                     device_id=(col, row), device_id_type=MESH).wait_recv()
        use(c)
        return 0

    lax.fori_loop(0, C - 1, arrive, 0)

    eu_j[...] = eu0[...] + acc[...].astype(BF16)

    def partial_j(c, _):
        cz, cy = c // Y, c % Y
        val = jnp.dot(slab_t[c], eu_j[...], preferred_element_type=F32)
        for i in range(R):
            p_j[i % 2, cy * X + i // 2, cz] = val[i * SH:(i + 1) * SH]
        return 0

    lax.fori_loop(0, C, partial_j, 0)

    def scatter_d(p, rd, sem):
        remote(p.at[1 - core], rd, sem, mate, col).start()

    def scatter_q(p, rd, s1, rxy, sem):
        await_recv(rd, sem)

        def fold(k):
            to = (q + k) % Q
            s1[to] = p[core, to] + rd[to]

        def go(k):
            to = (q + k) % Q
            r, c = q_to_rc(to)
            remote(s1.at[to], rxy.at[q], sem + 1, r, c).start()

        def both(k, _):
            fold(k)
            go(k - 1)
            return 0

        fold(1)
        lax.fori_loop(2, Q, both, 0)
        go(Q - 1)
        rxy[q] = p[core, q] + rd[q]

    def scatter_z(rxy, s2, rz, sem):
        await_recv(rxy.at[pl.ds(0, Q - 1)], sem + 1)

        def fold(to):
            return lax.fori_loop(1, Q, lambda k, t: t + rxy[k, to], rxy[0, to])

        def go(k):
            to = (z + k) % Z
            remote(s2.at[to], rz.at[z], sem + 2, row, to * Y + y).start()

        def both(k, _):
            to = (z + k) % Z
            s2[to] = fold(to)
            go(k - 1)
            return 0

        s2[(z + 1) % Z] = fold((z + 1) % Z)
        lax.fori_loop(2, Z, both, 0)
        go(Z - 1)
        rz[z] = fold(z)

    def scatter_end(p, s1, s2, rz, sem):
        await_recv(rz.at[pl.ds(0, Z - 1)], sem + 2)
        await_send(p.at[0], sem)
        await_send(s1.at[pl.ds(0, Q - 1)], sem + 1)
        await_send(s2.at[pl.ds(0, Z - 1)], sem + 2)
        return lax.fori_loop(1, Z, lambda k, t: t + rz[k], rz[0])

    scatter_d(p_j, rd_j, 7)
    scatter_q(p_j, rd_j, s1_j, rxy_j, 7)
    scatter_z(rxy_j, s2_j, rz_j, 7)
    mid_item = scatter_end(p_j, s1_j, s2_j, rz_j, 7).astype(BF16)

    tbl_j[core, q, z] = mid_item
    gather_z(tbl_j, 10)
    gather_q(tbl_j, 10)
    gather_d(tbl_j, 10)
    gather_end(tbl_j, 10)

    acc[...] = jnp.zeros_like(acc)

    def absorb(c, _):
        acc[...] += jnp.dot(slab[c], rows_of(tbl_j, c), preferred_element_type=F32)
        return 0

    lax.fori_loop(0, C, absorb, 0)

    def swap(v):
        return pltpu.roll(v, FEAT, 1)

    late_user = acc[...].astype(BF16).astype(F32)
    early_user = eu_j[...].astype(F32)
    sum_user = ((early_user + swap(early_user)) + late_user) + swap(late_user)
    user_rows = (sum_user / (LAYERS + 1)).astype(BF16)
    out_user[...] = user_rows[:, :FEAT]
    left = lax.broadcasted_iota(jnp.int32, late_user.shape, 1) < FEAT
    eu_2[...] = jnp.where(left, late_user, swap(late_user)).astype(BF16)

    ids = lax.broadcasted_iota(jnp.int32, (UD, TRIPLES), 0) + (row * C + col) * UD
    hit = (ids == trip[0:1, :]).astype(BF16)
    pk_z[z] = lax.dot_general(user_rows, hit, (((0,), (0,)), ((), ())), preferred_element_type=F32)[:FEAT].astype(BF16)

    def pick_z(k, _):
        remote(pk_z.at[z], pk_z.at[z], 16, row, ((z + k) % Z) * Y + y).start()
        return 0

    def pick_q(k, _):
        r, c = q_to_rc((q + k) % Q)
        remote(pk_q.at[q], pk_q.at[q], 17, r, c).start()
        return 0

    lax.fori_loop(1, Z, pick_z, 0)

    lane_left = lax.broadcasted_iota(jnp.int32, (HS, 2 * FEAT), 1) < FEAT

    def partial_3(c, _):
        cz, cy = c // Y, c % Y
        val = jnp.dot(slab_t[c], eu_2[...], preferred_element_type=F32)
        for i in range(R):
            p_3[i % 2, cy * X + i // 2, cz] = jnp.where(lane_left, val[i * SH:i * SH + HS], val[i * SH + HS:(i + 1) * SH])
        return 0

    lax.fori_loop(0, C, partial_3, 0)
    scatter_d(p_3, rd_3, 13)
    scatter_q(p_3, rd_3, s1_3, rxy_3, 13)
    await_recv(pk_z.at[pl.ds(0, Z - 1)], 16)
    pk_q[q] = lax.fori_loop(1, Z, lambda k, t: t + pk_z[k].astype(F32), pk_z[0].astype(F32)).astype(BF16)
    lax.fori_loop(1, Q, pick_q, 0)
    scatter_z(rxy_3, s2_3, rz_3, 13)
    await_recv(pk_q.at[pl.ds(0, Q - 1)], 17)
    pk_d[core] = lax.fori_loop(1, Q, lambda k, t: t + pk_q[k].astype(F32), pk_q[0].astype(F32)).astype(BF16)
    remote(pk_d.at[core], pk_d.at[core], 18, mate, col).start()
    last = scatter_end(p_3, s1_3, s2_3, rz_3, 13).astype(BF16).astype(F32)
    last_item = jnp.concatenate([last, swap(last)], axis=0)
    early_item = ei0[...].astype(F32)
    mid = mid_item.astype(F32)
    item_rows = (((swap(early_item) + mid) + swap(mid)) + last_item) / (LAYERS + 1)
    item_rows = item_rows.astype(BF16)[:, :FEAT]
    out_item[...] = item_rows

    await_recv(pk_d.at[0], 18)
    user_vec = (pk_d[0].astype(F32) + pk_d[1].astype(F32)).astype(BF16)
    dots = jnp.dot(item_rows, user_vec, preferred_element_type=F32)
    own = lax.broadcasted_iota(jnp.int32, (SH, TRIPLES), 0) + (col * R + row) * SH
    pos = jnp.sum(jnp.where(own == trip[1:2, :], dots, 0.0), axis=0, keepdims=True)
    neg = jnp.sum(jnp.where(own == trip[2:3, :], dots, 0.0), axis=0, keepdims=True)
    xc[col] = pos - neg

    def margin_col(k, _):
        remote(xc.at[col], xc.at[col], 19, row, (col + k) % C).start()
        return 0

    def margin_row(k, _):
        remote(xr.at[row], xr.at[row], 20, (row + k) % R, col).start()
        return 0

    lax.fori_loop(1, C, margin_col, 0)
    await_recv(xc.at[pl.ds(0, C - 1)], 19)
    xr[row] = lax.fori_loop(1, C, lambda k, t: t + xc[k], xc[0])
    lax.fori_loop(1, R, margin_row, 0)
    await_recv(xr.at[pl.ds(0, R - 1)], 20)
    margin = lax.fori_loop(1, R, lambda k, t: t + xr[k], xr[0])
    soft = jnp.maximum(-margin, 0.0) + jnp.log1p(jnp.exp(-jnp.abs(margin)))
    loss[...] = jnp.sum(soft, axis=1, keepdims=True) / TRIPLES

    await_send(deg_s.at[pl.ds(0, C - 1)], 0)
    await_send(ideg.at[pl.ds(0, R - 1)], 1)
    await_send(deg_f.at[pl.ds(0, C - 1)], 2)
    await_send(send_a.at[pl.ds(0, C - 1)], 3)
    await_send(pk_z.at[pl.ds(0, Z - 1)], 16)
    await_send(pk_q.at[pl.ds(0, Q - 1)], 17)
    await_send(pk_d.at[0], 18)
    await_send(xc.at[pl.ds(0, C - 1)], 19)
    await_send(xr.at[pl.ds(0, R - 1)], 20)


def build(mesh, Y, SH, UD):
    C, R = mesh.shape["col"], mesh.shape["row"]
    Z, X = C // Y, R // 2
    Q, IB, W = Y * X, R * SH, 2 * FEAT
    HS = SH // 2
    vm = pltpu.VMEM
    scratch = [
        vm((C, 1, UD), F32), vm((C, 1, UD), F32), vm((C, 1, UD), F32), vm((1, UD), F32), vm((R, 1, IB), F32),
        vm((C, UD, IB), BF16), vm((C, UD, IB), BF16), vm((C, IB, UD), BF16),
        vm((2, Q, Z, SH, W), BF16), vm((2, Q, Z, SH, W), BF16),
        vm((UD, W), F32), vm((UD, W), BF16), vm((UD, W), BF16),
        vm((2, Q, Z, SH, W), F32), vm((Q, Z, SH, W), F32), vm((Q, Z, SH, W), F32), vm((Q, Z, SH, W), F32),
        vm((Z, SH, W), F32), vm((Z, SH, W), F32),
        vm((2, Q, Z, HS, W), F32), vm((Q, Z, HS, W), F32), vm((Q, Z, HS, W), F32), vm((Q, Z, HS, W), F32),
        vm((Z, HS, W), F32), vm((Z, HS, W), F32),
        vm((Z, FEAT, TRIPLES), BF16), vm((Q, FEAT, TRIPLES), BF16), vm((2, FEAT, TRIPLES), BF16),
        vm((C, 1, TRIPLES), F32), vm((R, 1, TRIPLES), F32),
        pltpu.SemaphoreType.DMA((21,)), pltpu.SemaphoreType.DMA((21,)), pltpu.SemaphoreType.DMA((C,)),
    ]
    dims = (Z, Y, X, SH, UD)

    def local_prog(mask_blk, user_shard, item_shard, triples):
        out_user, out_item, loss = pl.pallas_call(
            functools.partial(kernel, dims),
            out_shape=(
                jax.ShapeDtypeStruct((UD, FEAT), BF16),
                jax.ShapeDtypeStruct((SH, FEAT), BF16),
                jax.ShapeDtypeStruct((1, 1), F32),
            ),
            in_specs=[pl.BlockSpec(memory_space=pltpu.VMEM)] * 4,
            out_specs=(pl.BlockSpec(memory_space=pltpu.VMEM),) * 3,
            scratch_shapes=scratch,
            compiler_params=pltpu.CompilerParams(
                collective_id=0, has_side_effects=True, vmem_limit_bytes=60 * 1024 * 1024),
            name="lightgcn",
        )(
            mask_blk.reshape(C, UD, IB),
            jnp.pad(user_shard, ((0, 0), (0, FEAT))),
            jnp.pad(item_shard, ((0, 0), (FEAT, 0))),
            triples.T,
        )
        return out_user, out_item, loss[0, 0]

    return jax.shard_map(
        local_prog, mesh=mesh,
        in_specs=(P("row", "col"), P(("row", "col"), None), P(("col", "row"), None), P(None, None)),
        out_specs=(P(("row", "col"), None), P(("col", "row"), None), P()), check_vma=False)


def solution(mesh):
    return build(mesh, Y=4, SH=16, UD=256)
```

time: 1380 us -> 169 us (0.12)
  waiting for transfers between devices: 1130 us -> 0 us
  blocking collectives: 200 us -> 0 us
  Pallas kernels: 0 us -> 161 us
  matrix products: 14.4 us -> 0 us
  other arithmetic: 14 us -> 0 us
    reduce_scatter x6 -> x0, waiting for transfers between devices: 719 us -> none  [the longest x3 629 us: local_prog(): lax.psum_scatter(user_part, 'col', scatter_dimension=0, tiled=True)]
    psum x1 -> x0, waiting for transfers between devices: 268 us -> none  [local_prog(): picked = lax.psum(picked, ('row', 'col'))]
    pallas_call x0 -> x1, Pallas kernels: none -> 161 us  [local_prog(): pl.pallas_call(functools.partial(kernel, dims), out_shape=(jax.ShapeDtype...]
    all_gather x3 -> x0, waiting for transfers between devices: 140 us -> none  [local_prog(): user_panel = lax.all_gather(layer_user, 'col', axis=0, tiled=True)]
    psum x2 -> x0, blocking collectives: 127 us -> none  [the longest x1 119 us: local_prog(): deg_user = jnp.maximum(lax.psum(jnp.sum(mask_blk, axis=1), 'col'), 1)]
    all_gather x3 -> x0, blocking collectives: 72.6 us -> none  [local_prog(): item_panel = lax.all_gather(layer_item, 'row', axis=0, tiled=True)]
    dot_general x6 -> x0, matrix products: 14.4 us -> none  [the longest x3 7.76 us: local_prog(): lax.dot_general(norm_adj, user_panel, (((0,), (0,)), ((), ())), preferred...]
  transfers between devices with their start and end apart: 10 -> 0, of which waited for: 9 -> 0; matrix products, arithmetic and copies ran while one was open for 2% -> 0% of each run, Pallas kernels for 0% -> 0%
where the time goes in v1:
time: 169 us
  Pallas kernels  161 us (95%)
  local copies, waits for them, and re-layouts  5.69 us (3%)
  between operations  2.4 us (1%)
    pallas_call x1, Pallas kernels, local_prog(): pl.pallas_call(functools.partial(kernel, dims), out_shape=(jax.ShapeDtype...  161 us
    unnamed x3, local copies, waits for them, and re-layouts  3.69 us

profile of v1, /device:TPU:1, one launch (start us, length us, event | category | flops | bytes accessed | tf_op | source)
XLA Modules:
  0.0 168.9 jit_solution(13304334883804826166)
XLA Ops:
  0.6 1.4 pad.9.ei0
  2.0 0.9 copy.7
  2.9 0.6 pad.8.eu0
  3.5 160.8 %lightgcn.1 = (bf16[256,64]{1,0:T(8,128)(2,1)}, bf16[16,64]{1,0:T(8,128)(2,1)}, f32[1,1]{1,0:T(1,128)}) custom-call(s32[32,256,128]{2,1,0:T(8,128)} %bitcast.3, bf16[256,128]{1,0:T(8,128)(2,1)} %pad.8.eu0, bf16[16,128]{1,0:T(8,128)(2,1)} %pad.9.ei0, s32[3,128]{1,0:T(4,128)} %bitcast.4), custom_call_target="tpu_custom_call" | custom-call | tf_op jit(solution)/shard_map/lightgcn/pallas_call | solution.py:382
  164.3 1.5 copy.8
  165.9 1.3 copy.11

commit v2 on v0

v2 whole, which is shorter than its diff:
```python
import functools

import jax
import jax.numpy as jnp
from jax import lax
from jax.experimental import pallas as pl
from jax.experimental.pallas import tpu as pltpu
from jax.sharding import PartitionSpec as P

MESH = pl.DeviceIdType.MESH
F32 = jnp.float32
BF16 = jnp.bfloat16
FEAT = 64
WIDE = 2 * FEAT
TRIPLES = 128
LAYERS = 3

DEG, IDEG, SPREAD, ATOA, GATHER0, GATHER1, GATHER2, PICK, MARGIN, SCATTER1 = 0, 1, 2, 3, 4, 7, 10, 13, 16, 18


def swap(v):
    return pltpu.roll(v, FEAT, 1)


def kernel(dims, mask, eu0, ei0, trip, out_user, out_item, loss, *scratch):
    Z, Y, X, SH, UD, G2 = dims
    C, R, Q = Z * Y, 2 * X, Y * X
    IB = R * SH
    HS = SH // 2
    (deg_s, deg_r, deg_f, own_deg, ideg, send_a, slab, slab_t, tbl0, tbl1, tbl2, acc, ed0, ed1, ed2, pk_z, pk_q, pk_d, xc, xr,
     sends, recvs, a2a_recv) = scratch[:23]
    groups = (Z, G2, G2)
    rs = [scratch[23 + 6 * n:29 + 6 * n] for n in range(3)]
    base = [SCATTER1]
    for n in range(3):
        base.append(base[-1] + 2 * groups[n] + 1)
    row = lax.axis_index("row")
    col = lax.axis_index("col")
    core, x = row % 2, row // 2
    z, y = col // Y, col % Y
    q = y * X + x
    mate = x * 2 + (1 - core)

    def remote(src, dst, sem, r, c, recv=None):
        return pltpu.make_async_remote_copy(
            src_ref=src, dst_ref=dst, send_sem=sends.at[sem], recv_sem=recvs.at[sem] if recv is None else recv,
            device_id=(c, r), device_id_type=MESH)

    def await_recv(ref, sem):
        remote(ref, ref, sem, row, col).wait_recv()

    def await_send(ref, sem):
        remote(ref, ref, sem, row, col).wait_send()

    def at_q(p):
        return (p % X) * 2 + core, z * Y + p // X

    def each(lo, hi, fn):
        lax.fori_loop(lo, hi, lambda k, t: (fn(k), t)[1], 0)

    barrier = pltpu.get_barrier_semaphore()

    def hail(c, r):
        pl.semaphore_signal(barrier, inc=1, device_id=(c, r), device_id_type=MESH)

    each(1, C, lambda k: hail((col + k) % C, row))
    each(1, R, lambda k: hail(col, (row + k) % R))
    each(0, (X - 1) * (Y - 1), lambda k: hail(z * Y + (y + 1 + k // (X - 1)) % Y, ((x + 1 + k % (X - 1)) % X) * 2 + core))

    ones = jnp.ones((8, IB), BF16)

    def count(k, part):
        blk = mask[k].astype(F32)
        sums = lax.dot_general(ones, blk.astype(BF16), (((1,), (1,)), ((), ())), preferred_element_type=F32)
        deg_s[k] = sums[0:1]
        return part + jnp.sum(blk.reshape(UD // 8, 8, IB), axis=0)

    part = lax.fori_loop(0, C, count, jnp.zeros((8, IB), F32), unroll=4)
    ideg[row] = jnp.sum(part, axis=0, keepdims=True)
    deg_r[col] = deg_s[col]

    lane_left = lax.broadcasted_iota(jnp.int32, (HS, WIDE), 1) < FEAT

    def pack(v):
        return jnp.where(lane_left, v[:HS], swap(v[HS:]))

    e0 = ei0[...].astype(F32)
    item0 = pack(jnp.concatenate([e0, jnp.zeros_like(e0)], axis=1))
    tbl0[core, q, z] = item0.astype(BF16)
    user0 = eu0[...].astype(F32)
    ed0[...] = jnp.transpose(jnp.concatenate([user0, user0], axis=0)).astype(BF16)
    pl.semaphore_wait(barrier, (C - 1) + (R - 1) + (X - 1) * (Y - 1))

    def gather_z(tbl, sem):
        each(1, Z, lambda k: remote(tbl.at[core, q, z], tbl.at[core, q, z], sem, row, ((z + k) % Z) * Y + y).start())

    def gather_q(tbl, sem):
        await_recv(tbl.at[core, q, pl.ds(0, Z - 1)], sem)
        each(1, Q, lambda k: remote(tbl.at[core, q], tbl.at[core, q], sem + 1, *at_q((q + k) % Q)).start())

    def gather_d(tbl, sem):
        await_recv(tbl.at[core, pl.ds(0, Q - 1)], sem + 1)
        remote(tbl.at[core], tbl.at[core], sem + 2, mate, col).start()

    def gather_end(tbl, sem):
        await_recv(tbl.at[core], sem + 2)

    def gather_sent(tbl, sem):
        await_send(tbl.at[core, q, pl.ds(0, Z - 1)], sem)
        await_send(tbl.at[core, pl.ds(0, Q - 1)], sem + 1)
        await_send(tbl.at[core], sem + 2)

    def rows_of(tbl, c):
        cz, cy = c // Y, c % Y
        parts = []
        for i in range(R):
            v = tbl[i % 2, cy * X + i // 2, cz].astype(F32)
            parts += [v, swap(v)]
        return jnp.concatenate(parts, axis=0).astype(BF16)

    each(1, C, lambda k: remote(deg_s.at[(col + k) % C], deg_r.at[col], DEG, row, (col + k) % C).start())
    each(1, R, lambda k: remote(ideg.at[row], ideg.at[row], IDEG, (row + k) % R, col).start())
    gather_z(tbl0, GATHER0)
    await_recv(deg_r.at[pl.ds(0, C - 1)], DEG)
    own_deg[...] = lax.fori_loop(0, C, lambda k, t: t + deg_r[k], jnp.zeros((1, UD), F32), unroll=True)
    deg_f[col] = own_deg[...]
    each(1, C, lambda k: remote(own_deg, deg_f.at[col], SPREAD, row, (col + k) % C).start())
    await_recv(ideg.at[pl.ds(0, R - 1)], IDEG)
    scale_item = lax.rsqrt(jnp.maximum(lax.fori_loop(0, R, lambda k, t: t + ideg[k], jnp.zeros((1, IB), F32), unroll=True), 1.0))
    gather_q(tbl0, GATHER0)
    await_recv(deg_f.at[pl.ds(0, C - 1)], SPREAD)

    def order(k):
        j, dy = k // Y, (k + 1) % Y
        m = Z // 2 - (j + 1) // 2
        odd = j % 2
        return (odd * m + (1 - odd) * (Z - m)) % Z, dy

    def piece(c):
        scale = lax.rsqrt(jnp.maximum(deg_f[c], 1.0))
        scale = jnp.transpose(jnp.broadcast_to(scale, (IB, UD)))
        return (mask[c].astype(F32) * scale * scale_item).astype(BF16)

    def target(k):
        dz, dy = order(k)
        return ((z + dz) % Z) * Y + (y + dy) % Y

    def ship(k):
        to = target(k)
        remote(send_a.at[to], slab.at[col], ATOA, row, to, recv=a2a_recv.at[col]).start()

    send_a[target(0)] = piece(target(0))

    def make_and_ship(k):
        send_a[target(k)] = piece(target(k))
        ship(k - 1)

    each(1, C - 1, make_and_ship)
    slab[col] = piece(col)
    ship(C - 2)
    gather_d(tbl0, GATHER0)
    gather_end(tbl0, GATHER0)

    def scatter_a(n, g, ed):
        p, rd = rs[n][0], rs[n][1]
        per = Z // groups[n]

        def block(k):
            zi, cy = k // Y, k % Y
            val = jnp.dot(slab_t[(g * per + zi) * Y + cy], ed[...], preferred_element_type=F32)
            for i in range(R):
                p[i % 2, g, cy * X + i // 2, zi] = jnp.where(lane_left, val[i * SH:i * SH + HS], val[i * SH + HS:(i + 1) * SH])

        lax.fori_loop(0, per * Y, lambda k, t: (block(k), t)[1], 0, unroll=4)
        remote(p.at[1 - core, g], rd.at[g], base[n], mate, col, recv=recvs.at[base[n] + g]).start()

    def scatter_b(n, g):
        p, rd, s1, rxy, _, _ = rs[n]
        remote(rd.at[g], rd.at[g], base[n], row, col, recv=recvs.at[base[n] + g]).wait_recv()

        def fold(k):
            to = (q + k) % Q
            s1[g, to] = p[core, g, to] + rd[g, to]

        def go(k):
            to = (q + k) % Q
            remote(s1.at[g, to], rxy.at[g, q], base[n] + 1, *at_q(to), recv=recvs.at[base[n] + groups[n] + g]).start()

        def both(k):
            fold(k)
            go(k - 1)

        fold(1)
        each(2, Q, both)
        rxy[g, q] = p[core, g, q] + rd[g, q]
        go(Q - 1)

    def scatter_c(n, g):
        _, _, _, rxy, s2, rz = rs[n]
        per = Z // groups[n]
        part = rxy.at[g, pl.ds(0, Q - 1)]
        remote(part, part, base[n], row, col, recv=recvs.at[base[n] + groups[n] + g]).wait_recv()
        for zi in range(per):
            to = g * per + zi
            s2[to] = lax.fori_loop(1, Q, lambda k, t: t + rxy[g, k, zi], rxy[g, 0, zi], unroll=True)
        for zi in range(per):
            to = g * per + zi

            @pl.when(to != z)
            def _():
                remote(s2.at[to], rz.at[z], base[n] + 2, row, to * Y + y, recv=recvs.at[base[n] + 2 * groups[n]]).start()

            @pl.when(to == z)
            def _():
                rz[z] = s2[to]

    def scatter_end(n):
        rz = rs[n][5]
        part = rz.at[pl.ds(0, Z - 1)]
        remote(part, part, base[n], row, col, recv=recvs.at[base[n] + 2 * groups[n]]).wait_recv()
        return lax.fori_loop(1, Z, lambda k, t: t + rz[k], rz[0], unroll=True).astype(BF16)

    def scatter_sent(n):
        p, _, s1, _, s2, _ = rs[n]
        await_send(p.at[0], base[n])
        await_send(s1.at[:, pl.ds(0, Q - 1)], base[n] + 1)
        await_send(s2.at[pl.ds(0, Z - 1)], base[n] + 2)

    def source(k):
        dz, dy = order(k)
        return ((z - dz + Z) % Z) * Y + (y - dy + Y) % Y

    def use(c):
        blk = slab[c]
        slab_t[c] = jnp.transpose(blk)
        acc[...] += jnp.dot(blk, rows_of(tbl0, c), preferred_element_type=F32)

    def arrive(k):
        c = source(k)
        pltpu.make_async_remote_copy(src_ref=slab.at[c], dst_ref=slab.at[c], send_sem=sends.at[ATOA], recv_sem=a2a_recv.at[c],
                                     device_id=(col, row), device_id_type=MESH).wait_recv()
        use(c)

    def group(j):
        return source(j * Y) // Y

    acc[...] = jnp.zeros_like(acc)
    use(col)

    def stream(j):
        each(j * Y, (j + 1) * Y, arrive)
        scatter_a(0, group(j), ed0)

        @pl.when(j >= 1)
        def _():
            scatter_b(0, group(j - 1))

        @pl.when(j >= 2)
        def _():
            scatter_c(0, group(j - 2))

    each(0, Z - 1, stream)
    each((Z - 1) * Y, C - 1, arrive)
    scatter_a(0, z, ed0)
    wide_left = lax.broadcasted_iota(jnp.int32, (UD, WIDE), 1) < FEAT

    def twice(v):
        return jnp.where(wide_left, v, swap(v)).astype(BF16)

    user1 = acc[...].astype(BF16).astype(F32)
    ed1[...] = twice(user1)
    for g in range(G2):
        scatter_a(1, g, ed1)
        if g == 0:
            scatter_b(0, group(Z - 2))
            scatter_b(0, z)
    if Z > 2:
        scatter_c(0, group(Z - 3))
    scatter_c(0, group(Z - 2))
    for g in range(G2):
        scatter_b(1, g)
    scatter_c(0, z)
    item1 = scatter_end(0)
    tbl1[core, q, z] = item1
    gather_z(tbl1, GATHER1)
    for g in range(G2):
        scatter_c(1, g)
        if g == G2 // 2 - 1:
            gather_q(tbl1, GATHER1)
    item2 = scatter_end(1)
    tbl2[core, q, z] = item2
    gather_z(tbl2, GATHER2)
    gather_d(tbl1, GATHER1)
    gather_q(tbl2, GATHER2)
    gather_end(tbl1, GATHER1)

    def absorb(tbl):
        acc[...] = jnp.zeros_like(acc)

        def step(c):
            acc[...] += jnp.dot(slab[c], rows_of(tbl, c), preferred_element_type=F32)

        lax.fori_loop(0, C, lambda k, t: (step(k), t)[1], 0, unroll=4)
        return acc[...].astype(BF16).astype(F32)

    user2 = absorb(tbl1)
    ed2[...] = twice(user2)
    for g in range(G2):
        scatter_a(2, g, ed2)
        if g > 0:
            scatter_b(2, g - 1)
    scatter_b(2, G2 - 1)
    gather_d(tbl2, GATHER2)
    gather_end(tbl2, GATHER2)
    user3 = absorb(tbl2)
    sum_user = ((ed0[...].astype(F32) + ed1[...].astype(F32)) + ed2[...].astype(F32)) + user3
    user_rows = (sum_user / (LAYERS + 1)).astype(BF16)

    ids = lax.broadcasted_iota(jnp.int32, (UD, TRIPLES), 0) + (row * C + col) * UD
    hit = (ids == trip[0:1, :]).astype(BF16)
    pk_z[z] = lax.dot_general(user_rows, hit, (((0,), (0,)), ((), ())), preferred_element_type=F32)[:FEAT].astype(BF16)
    each(1, Z, lambda k: remote(pk_z.at[z], pk_z.at[z], PICK, row, ((z + k) % Z) * Y + y).start())
    out_user[...] = jnp.transpose(user_rows.astype(F32))[:FEAT].astype(BF16)

    for g in range(G2):
        scatter_c(2, g)
    await_recv(pk_z.at[pl.ds(0, Z - 1)], PICK)
    pk_q[q] = lax.fori_loop(1, Z, lambda k, t: t + pk_z[k].astype(F32), pk_z[0].astype(F32)).astype(BF16)
    each(1, Q, lambda k: remote(pk_q.at[q], pk_q.at[q], PICK + 1, *at_q((q + k) % Q)).start())
    item3 = scatter_end(2)
    sum_item = ((item0 + item1.astype(F32)) + item2.astype(F32)) + item3.astype(F32)
    packed = (sum_item / (LAYERS + 1)).astype(BF16).astype(F32)
    item_rows = jnp.concatenate([packed, swap(packed)], axis=0).astype(BF16)[:, :FEAT]
    out_item[...] = item_rows

    await_recv(pk_q.at[pl.ds(0, Q - 1)], PICK + 1)
    pk_d[core] = lax.fori_loop(1, Q, lambda k, t: t + pk_q[k].astype(F32), pk_q[0].astype(F32)).astype(BF16)
    remote(pk_d.at[core], pk_d.at[core], PICK + 2, mate, col).start()
    await_recv(pk_d.at[0], PICK + 2)
    user_vec = (pk_d[0].astype(F32) + pk_d[1].astype(F32)).astype(BF16)
    dots = jnp.dot(item_rows, user_vec, preferred_element_type=F32)
    own = lax.broadcasted_iota(jnp.int32, (SH, TRIPLES), 0) + (col * R + row) * SH
    pos = jnp.sum(jnp.where(own == trip[1:2, :], dots, 0.0), axis=0, keepdims=True)
    neg = jnp.sum(jnp.where(own == trip[2:3, :], dots, 0.0), axis=0, keepdims=True)
    xc[col] = pos - neg
    each(1, C, lambda k: remote(xc.at[col], xc.at[col], MARGIN, row, (col + k) % C).start())
    await_recv(xc.at[pl.ds(0, C - 1)], MARGIN)
    xr[row] = lax.fori_loop(1, C, lambda k, t: t + xc[k], xc[0], unroll=True)
    each(1, R, lambda k: remote(xr.at[row], xr.at[row], MARGIN + 1, (row + k) % R, col).start())
    await_recv(xr.at[pl.ds(0, R - 1)], MARGIN + 1)
    margin = lax.fori_loop(1, R, lambda k, t: t + xr[k], xr[0], unroll=True)
    soft = jnp.maximum(-margin, 0.0) + jnp.log1p(jnp.exp(-jnp.abs(margin)))
    loss[...] = jnp.sum(soft, axis=1, keepdims=True) / TRIPLES

    await_send(deg_s.at[pl.ds(0, C - 1)], DEG)
    await_send(ideg.at[pl.ds(0, R - 1)], IDEG)
    await_send(deg_f.at[pl.ds(0, C - 1)], SPREAD)
    await_send(send_a.at[pl.ds(0, C - 1)], ATOA)
    gather_sent(tbl0, GATHER0)
    gather_sent(tbl1, GATHER1)
    gather_sent(tbl2, GATHER2)
    for n in range(3):
        scatter_sent(n)
    await_send(pk_z.at[pl.ds(0, Z - 1)], PICK)
    await_send(pk_q.at[pl.ds(0, Q - 1)], PICK + 1)
    await_send(pk_d.at[0], PICK + 2)
    await_send(xc.at[pl.ds(0, C - 1)], MARGIN)
    await_send(xr.at[pl.ds(0, R - 1)], MARGIN + 1)


def build(mesh, Y, SH, UD, G2):
    C, R = mesh.shape["col"], mesh.shape["row"]
    Z, X = C // Y, R // 2
    Q, IB, HS = Y * X, R * SH, SH // 2
    vm = pltpu.VMEM
    scratch = [
        vm((C, 1, UD), F32), vm((C, 1, UD), F32), vm((C, 1, UD), F32), vm((1, UD), F32), vm((R, 1, IB), F32),
        vm((C, UD, IB), BF16), vm((C, UD, IB), BF16), vm((C, IB, UD), BF16),
        vm((2, Q, Z, HS, WIDE), BF16), vm((2, Q, Z, HS, WIDE), BF16), vm((2, Q, Z, HS, WIDE), BF16),
        vm((UD, WIDE), F32), vm((UD, WIDE), BF16), vm((UD, WIDE), BF16), vm((UD, WIDE), BF16),
        vm((Z, FEAT, TRIPLES), BF16), vm((Q, FEAT, TRIPLES), BF16), vm((2, FEAT, TRIPLES), BF16),
        vm((C, 1, TRIPLES), F32), vm((R, 1, TRIPLES), F32),
    ]
    count = SCATTER1 + sum(2 * g + 1 for g in (Z, G2, G2)) + 1
    scratch += [pltpu.SemaphoreType.DMA((count,)), pltpu.SemaphoreType.DMA((count,)), pltpu.SemaphoreType.DMA((C,))]
    for g in (Z, G2, G2):
        scratch += [vm((2, g, Q, Z // g, HS, WIDE), F32)] + [vm((g, Q, Z // g, HS, WIDE), F32)] * 3 + [vm((Z, HS, WIDE), F32)] * 2
    dims = (Z, Y, X, SH, UD, G2)

    def local_prog(mask_blk, user_shard, item_shard, triples):
        out_user, out_item, loss = pl.pallas_call(
            functools.partial(kernel, dims),
            out_shape=(
                jax.ShapeDtypeStruct((FEAT, UD), BF16),
                jax.ShapeDtypeStruct((SH, FEAT), BF16),
                jax.ShapeDtypeStruct((1, 1), F32),
            ),
            in_specs=[pl.BlockSpec(memory_space=pltpu.VMEM)] * 4,
            out_specs=(pl.BlockSpec(memory_space=pltpu.VMEM),) * 3,
            scratch_shapes=scratch,
            compiler_params=pltpu.CompilerParams(
                collective_id=0, has_side_effects=True, vmem_limit_bytes=60 * 1024 * 1024),
            name="lightgcn",
        )(mask_blk.reshape(C, UD, IB), user_shard.T, item_shard, triples.T)
        return out_user.T, out_item, loss[0, 0]

    return jax.shard_map(
        local_prog, mesh=mesh,
        in_specs=(P("row", "col"), P(("row", "col"), None), P(("col", "row"), None), P(None, None)),
        out_specs=(P(("row", "col"), None), P(("col", "row"), None), P()), check_vma=False)


def solution(mesh):
    return build(mesh, Y=4, SH=16, UD=256, G2=4)
```

time: 1380 us -> 147 us (0.11)
  waiting for transfers between devices: 1130 us -> 0 us
  blocking collectives: 200 us -> 0 us
  Pallas kernels: 0 us -> 142 us
  matrix products: 14.4 us -> 0 us
  other arithmetic: 14 us -> 0 us
    reduce_scatter x6 -> x0, waiting for transfers between devices: 719 us -> none  [the longest x3 629 us: local_prog(): lax.psum_scatter(user_part, 'col', scatter_dimension=0, tiled=True)]
    psum x1 -> x0, waiting for transfers between devices: 268 us -> none  [local_prog(): picked = lax.psum(picked, ('row', 'col'))]
    pallas_call x0 -> x1, Pallas kernels: none -> 142 us  [local_prog(): pl.pallas_call(functools.partial(kernel, dims), out_shape=(jax.ShapeDtype...]
    all_gather x3 -> x0, waiting for transfers between devices: 140 us -> none  [local_prog(): user_panel = lax.all_gather(layer_user, 'col', axis=0, tiled=True)]
    psum x2 -> x0, blocking collectives: 127 us -> none  [the longest x1 119 us: local_prog(): deg_user = jnp.maximum(lax.psum(jnp.sum(mask_blk, axis=1), 'col'), 1)]
    all_gather x3 -> x0, blocking collectives: 72.6 us -> none  [local_prog(): item_panel = lax.all_gather(layer_item, 'row', axis=0, tiled=True)]
    dot_general x6 -> x0, matrix products: 14.4 us -> none  [the longest x3 7.76 us: local_prog(): lax.dot_general(norm_adj, user_panel, (((0,), (0,)), ((), ())), preferred...]
  transfers between devices with their start and end apart: 10 -> 0, of which waited for: 9 -> 0; matrix products, arithmetic and copies ran while one was open for 2% -> 0% of each run, Pallas kernels for 0% -> 0%
where the time goes in v2:
time: 147 us
  Pallas kernels  142 us (97%)
  local copies, waits for them, and re-layouts  2.65 us (2%)
  between operations  2.38 us (2%)
    pallas_call x1, Pallas kernels, local_prog(): pl.pallas_call(functools.partial(kernel, dims), out_shape=(jax.ShapeDtype...  142 us

profile of v2, /device:TPU:1, one launch (start us, length us, event | category | flops | bytes accessed | tf_op | source)
XLA Modules:
  0.0 147.1 jit_solution(11933215281657576663)
XLA Ops:
  0.6 142.1 %lightgcn.1 = (bf16[64,256]{1,0:T(8,128)(2,1)}, bf16[16,64]{1,0:T(8,128)(2,1)}, f32[1,1]{1,0:T(1,128)}) custom-call(s32[32,256,128]{2,1,0:T(8,128)} %bitcast.5, bf16[64,256]{1,0:T(8,128)(2,1)} %bitcast.6, bf16[16,64]{1,0:T(8,128)(2,1)} %ei0.1, s32[3,128]{1,0:T(4,128)} %bitcast.8), custom_call_target="tpu_custom_call" | custom-call | tf_op jit(solution)/shard_map/lightgcn/pallas_call | solution.py:391
  142.7 1.4 copy.10
  144.1 1.3 copy.11

commit v3 on v2

--- a/solution.py
+++ b/solution.py
@@ -14,23 +14,25 @@
 WIDE = 2 * FEAT
 TRIPLES = 128
 LAYERS = 3
-
-DEG, IDEG, SPREAD, ATOA, GATHER0, GATHER1, GATHER2, PICK, MARGIN, SCATTER1 = 0, 1, 2, 3, 4, 7, 10, 13, 16, 18
+LOADS = 8
+PICKS = TRIPLES // 4
+
+DEG, IDEG, SPREAD, ATOA, GATHER0, GATHER1, PICK, MARGIN, SCATTER1 = 0, 1, 2, 3, 4, 7, 10, 14, 16
 
 
 def swap(v):
     return pltpu.roll(v, FEAT, 1)
 
 
-def kernel(dims, mask, eu0, ei0, trip, out_user, out_item, loss, *scratch):
+def kernel(dims, mask_hbm, eu0, ei0, trip, out_user, out_item, loss, *scratch):
     Z, Y, X, SH, UD, G2 = dims
     C, R, Q = Z * Y, 2 * X, Y * X
     IB = R * SH
     HS = SH // 2
-    (deg_s, deg_r, deg_f, own_deg, ideg, send_a, slab, slab_t, tbl0, tbl1, tbl2, acc, ed0, ed1, ed2, pk_z, pk_q, pk_d, xc, xr,
-     sends, recvs, a2a_recv) = scratch[:23]
+    (deg_s, deg_r, deg_f, own_deg, ideg, send_a, slab, slab_t, tbl0, tbl1, acc, ed0, ed1, ed2, pk_a, pk_b, pk_z, pk_q, pk_d, xc, xr,
+     sends, recvs, a2a_recv, mask, load_sem) = scratch[:26]
     groups = (Z, G2, G2)
-    rs = [scratch[23 + 6 * n:29 + 6 * n] for n in range(3)]
+    rs = [scratch[26 + 6 * n:32 + 6 * n] for n in range(3)]
     base = [SCATTER1]
     for n in range(3):
         base.append(base[-1] + 2 * groups[n] + 1)
@@ -58,6 +60,15 @@
     def each(lo, hi, fn):
         lax.fori_loop(lo, hi, lambda k, t: (fn(k), t)[1], 0)
 
+    run = C // LOADS
+
+    def load(i):
+        part = pl.ds(i * run, run)
+        return pltpu.make_async_copy(mask_hbm.at[part], mask.at[part], load_sem.at[i])
+
+    for i in range(LOADS):
+        load(i).start()
+
     barrier = pltpu.get_barrier_semaphore()
 
     def hail(c, r):
@@ -75,7 +86,10 @@
         deg_s[k] = sums[0:1]
         return part + jnp.sum(blk.reshape(UD // 8, 8, IB), axis=0)
 
-    part = lax.fori_loop(0, C, count, jnp.zeros((8, IB), F32), unroll=4)
+    part = jnp.zeros((8, IB), F32)
+    for i in range(LOADS):
+        load(i).wait()
+        part = lax.fori_loop(i * run, (i + 1) * run, count, part, unroll=True)
     ideg[row] = jnp.sum(part, axis=0, keepdims=True)
     deg_r[col] = deg_s[col]
 
@@ -261,7 +275,6 @@
 
     each(0, Z - 1, stream)
     each((Z - 1) * Y, C - 1, arrive)
-    scatter_a(0, z, ed0)
     wide_left = lax.broadcasted_iota(jnp.int32, (UD, WIDE), 1) < FEAT
 
     def twice(v):
@@ -271,74 +284,82 @@
     ed1[...] = twice(user1)
     for g in range(G2):
         scatter_a(1, g, ed1)
-        if g == 0:
-            scatter_b(0, group(Z - 2))
-            scatter_b(0, z)
+        if g > 0:
+            scatter_b(1, g - 1)
+    scatter_a(0, z, ed0)
+    scatter_b(1, G2 - 1)
+    scatter_b(0, group(Z - 2))
+    scatter_b(0, z)
     if Z > 2:
         scatter_c(0, group(Z - 3))
+    scatter_c(1, 0)
     scatter_c(0, group(Z - 2))
-    for g in range(G2):
-        scatter_b(1, g)
     scatter_c(0, z)
-    item1 = scatter_end(0)
-    tbl1[core, q, z] = item1
+    for g in range(1, G2):
+        scatter_c(1, g)
+    item1 = scatter_end(0).astype(F32)
+    item2 = scatter_end(1).astype(F32)
+    low = jnp.where(lane_left, item1, swap(item2))
+    high = jnp.where(lane_left, swap(item1), item2)
+    tbl1[core, q, z] = jnp.concatenate([low, high], axis=0).astype(BF16)
     gather_z(tbl1, GATHER1)
-    for g in range(G2):
-        scatter_c(1, g)
-        if g == G2 // 2 - 1:
-            gather_q(tbl1, GATHER1)
-    item2 = scatter_end(1)
-    tbl2[core, q, z] = item2
-    gather_z(tbl2, GATHER2)
+    gather_q(tbl1, GATHER1)
     gather_d(tbl1, GATHER1)
-    gather_q(tbl2, GATHER2)
+    acc[...] = jnp.zeros_like(acc)
     gather_end(tbl1, GATHER1)
 
-    def absorb(tbl):
-        acc[...] = jnp.zeros_like(acc)
-
-        def step(c):
-            acc[...] += jnp.dot(slab[c], rows_of(tbl, c), preferred_element_type=F32)
-
-        lax.fori_loop(0, C, lambda k, t: (step(k), t)[1], 0, unroll=4)
-        return acc[...].astype(BF16).astype(F32)
-
-    user2 = absorb(tbl1)
-    ed2[...] = twice(user2)
-    for g in range(G2):
-        scatter_a(2, g, ed2)
-        if g > 0:
-            scatter_b(2, g - 1)
-    scatter_b(2, G2 - 1)
-    gather_d(tbl2, GATHER2)
-    gather_end(tbl2, GATHER2)
-    user3 = absorb(tbl2)
-    sum_user = ((ed0[...].astype(F32) + ed1[...].astype(F32)) + ed2[...].astype(F32)) + user3
+    def absorb(c):
+        cz, cy = c // Y, c % Y
+        rows = jnp.concatenate([tbl1[i % 2, cy * X + i // 2, cz] for i in range(R)], axis=0)
+        acc[...] += jnp.dot(slab[c], rows, preferred_element_type=F32)
+
+    lax.fori_loop(0, C, lambda k, t: (absorb(k), t)[1], 0, unroll=4)
+    late = acc[...].astype(BF16).astype(F32)
+    ed2[...] = twice(late)
+    scatter_a(2, 0, ed2)
+    sum_user = ((ed0[...].astype(F32) + ed1[...].astype(F32)) + ed2[...].astype(F32)) + jnp.where(wide_left, swap(late), late)
     user_rows = (sum_user / (LAYERS + 1)).astype(BF16)
 
     ids = lax.broadcasted_iota(jnp.int32, (UD, TRIPLES), 0) + (row * C + col) * UD
     hit = (ids == trip[0:1, :]).astype(BF16)
-    pk_z[z] = lax.dot_general(user_rows, hit, (((0,), (0,)), ((), ())), preferred_element_type=F32)[:FEAT].astype(BF16)
-    each(1, Z, lambda k: remote(pk_z.at[z], pk_z.at[z], PICK, row, ((z + k) % Z) * Y + y).start())
+    found = lax.dot_general(hit, user_rows, (((0,), (0,)), ((), ())), preferred_element_type=F32)
+    pick_left = lax.broadcasted_iota(jnp.int32, (PICKS, WIDE), 1) < FEAT
+    for h in range(2):
+        lo, hi = h * PICKS, (h + 2) * PICKS
+        pk_a[h] = jnp.where(pick_left, found[lo:lo + PICKS], found[hi:hi + PICKS]).astype(BF16)
+    remote(pk_a.at[1 - core], pk_b, PICK, mate, col).start()
+    for g in range(1, G2):
+        scatter_a(2, g, ed2)
+        if g == 1:
+            await_recv(pk_b, PICK)
+            pk_z[z] = (pk_a[core].astype(F32) + pk_b[...].astype(F32)).astype(BF16)
+            each(1, Z, lambda k: remote(pk_z.at[z], pk_z.at[z], PICK + 1, row, ((z + k) % Z) * Y + y).start())
+        scatter_b(2, g - 1)
+    scatter_b(2, G2 - 1)
     out_user[...] = jnp.transpose(user_rows.astype(F32))[:FEAT].astype(BF16)
-
+    await_recv(pk_z.at[pl.ds(0, Z - 1)], PICK + 1)
+    pk_q[q] = lax.fori_loop(1, Z, lambda k, t: t + pk_z[k].astype(F32), pk_z[0].astype(F32), unroll=True).astype(BF16)
+    each(1, Q, lambda k: remote(pk_q.at[q], pk_q.at[q], PICK + 2, *at_q((q + k) % Q)).start())
     for g in range(G2):
         scatter_c(2, g)
-    await_recv(pk_z.at[pl.ds(0, Z - 1)], PICK)
-    pk_q[q] = lax.fori_loop(1, Z, lambda k, t: t + pk_z[k].astype(F32), pk_z[0].astype(F32)).astype(BF16)
-    each(1, Q, lambda k: remote(pk_q.at[q], pk_q.at[q], PICK + 1, *at_q((q + k) % Q)).start())
+    await_recv(pk_q.at[pl.ds(0, Q - 1)], PICK + 2)
+    pk_d[core] = lax.fori_loop(1, Q, lambda k, t: t + pk_q[k].astype(F32), pk_q[0].astype(F32), unroll=True).astype(BF16)
+    remote(pk_d.at[core], pk_d.at[core], PICK + 3, mate, col).start()
     item3 = scatter_end(2)
-    sum_item = ((item0 + item1.astype(F32)) + item2.astype(F32)) + item3.astype(F32)
+    sum_item = ((item0 + item1) + item2) + item3.astype(F32)
     packed = (sum_item / (LAYERS + 1)).astype(BF16).astype(F32)
-    item_rows = jnp.concatenate([packed, swap(packed)], axis=0).astype(BF16)[:, :FEAT]
-    out_item[...] = item_rows
-
-    await_recv(pk_q.at[pl.ds(0, Q - 1)], PICK + 1)
-    pk_d[core] = lax.fori_loop(1, Q, lambda k, t: t + pk_q[k].astype(F32), pk_q[0].astype(F32)).astype(BF16)
-    remote(pk_d.at[core], pk_d.at[core], PICK + 2, mate, col).start()
-    await_recv(pk_d.at[0], PICK + 2)
-    user_vec = (pk_d[0].astype(F32) + pk_d[1].astype(F32)).astype(BF16)
-    dots = jnp.dot(item_rows, user_vec, preferred_element_type=F32)
+    zero = jnp.zeros_like(packed)
+    left_rows = [jnp.where(lane_left, packed, zero), jnp.where(lane_left, swap(packed), zero)]
+    right_rows = [jnp.where(lane_left, zero, swap(packed)), jnp.where(lane_left, zero, packed)]
+    item_rows = jnp.concatenate(left_rows, axis=0).astype(BF16)
+    out_item[...] = item_rows[:, :FEAT]
+
+    await_recv(pk_d.at[0], PICK + 3)
+    user_vec = jnp.concatenate([pk_d[0], pk_d[1], pk_d[0], pk_d[1]], axis=0)
+    nt = (((1,), (1,)), ((), ()))
+    dots_l = lax.dot_general(item_rows, user_vec, nt, preferred_element_type=F32)
+    dots_r = lax.dot_general(jnp.concatenate(right_rows, axis=0).astype(BF16), user_vec, nt, preferred_element_type=F32)
+    dots = jnp.where(lax.broadcasted_iota(jnp.int32, (SH, TRIPLES), 1) < TRIPLES // 2, dots_l, dots_r)
     own = lax.broadcasted_iota(jnp.int32, (SH, TRIPLES), 0) + (col * R + row) * SH
     pos = jnp.sum(jnp.where(own == trip[1:2, :], dots, 0.0), axis=0, keepdims=True)
     neg = jnp.sum(jnp.where(own == trip[2:3, :], dots, 0.0), axis=0, keepdims=True)
@@ -358,12 +379,12 @@
     await_send(send_a.at[pl.ds(0, C - 1)], ATOA)
     gather_sent(tbl0, GATHER0)
     gather_sent(tbl1, GATHER1)
-    gather_sent(tbl2, GATHER2)
     for n in range(3):
         scatter_sent(n)
-    await_send(pk_z.at[pl.ds(0, Z - 1)], PICK)
-    await_send(pk_q.at[pl.ds(0, Q - 1)], PICK + 1)
-    await_send(pk_d.at[0], PICK + 2)
+    await_send(pk_b, PICK)
+    await_send(pk_z.at[pl.ds(0, Z - 1)], PICK + 1)
+    await_send(pk_q.at[pl.ds(0, Q - 1)], PICK + 2)
+    await_send(pk_d.at[0], PICK + 3)
     await_send(xc.at[pl.ds(0, C - 1)], MARGIN)
     await_send(xr.at[pl.ds(0, R - 1)], MARGIN + 1)
 
@@ -376,13 +397,15 @@
     scratch = [
         vm((C, 1, UD), F32), vm((C, 1, UD), F32), vm((C, 1, UD), F32), vm((1, UD), F32), vm((R, 1, IB), F32),
         vm((C, UD, IB), BF16), vm((C, UD, IB), BF16), vm((C, IB, UD), BF16),
-        vm((2, Q, Z, HS, WIDE), BF16), vm((2, Q, Z, HS, WIDE), BF16), vm((2, Q, Z, HS, WIDE), BF16),
+        vm((2, Q, Z, HS, WIDE), BF16), vm((2, Q, Z, SH, WIDE), BF16),
         vm((UD, WIDE), F32), vm((UD, WIDE), BF16), vm((UD, WIDE), BF16), vm((UD, WIDE), BF16),
-        vm((Z, FEAT, TRIPLES), BF16), vm((Q, FEAT, TRIPLES), BF16), vm((2, FEAT, TRIPLES), BF16),
+        vm((2, PICKS, WIDE), BF16), vm((PICKS, WIDE), BF16),
+        vm((Z, PICKS, WIDE), BF16), vm((Q, PICKS, WIDE), BF16), vm((2, PICKS, WIDE), BF16),
         vm((C, 1, TRIPLES), F32), vm((R, 1, TRIPLES), F32),
     ]
     count = SCATTER1 + sum(2 * g + 1 for g in (Z, G2, G2)) + 1
-    scratch += [pltpu.SemaphoreType.DMA((count,)), pltpu.SemaphoreType.DMA((count,)), pltpu.SemaphoreType.DMA((C,))]
+    scratch += [pltpu.SemaphoreType.DMA((count,)), pltpu.SemaphoreType.DMA((count,)), pltpu.SemaphoreType.DMA((C,)),
+                vm((C, UD, IB), jnp.int32), pltpu.SemaphoreType.DMA((LOADS,))]
     for g in (Z, G2, G2):
         scratch += [vm((2, g, Q, Z // g, HS, WIDE), F32)] + [vm((g, Q, Z // g, HS, WIDE), F32)] * 3 + [vm((Z, HS, WIDE), F32)] * 2
     dims = (Z, Y, X, SH, UD, G2)
@@ -395,7 +418,7 @@
                 jax.ShapeDtypeStruct((SH, FEAT), BF16),
                 jax.ShapeDtypeStruct((1, 1), F32),
             ),
-            in_specs=[pl.BlockSpec(memory_space=pltpu.VMEM)] * 4,
+            in_specs=[pl.BlockSpec(memory_space=pl.ANY)] + [pl.BlockSpec(memory_space=pltpu.VMEM)] * 3,
             out_specs=(pl.BlockSpec(memory_space=pltpu.VMEM),) * 3,
             scratch_shapes=scratch,
             compiler_params=pltpu.CompilerParams(

time: 147 us -> 147 us (level)
  no operation moved by 1% of the time
where the time goes in v3:
time: 147 us; the launch traced here: 146 us
  Pallas kernels  141 us (96%)
  local copies, waits for them, and re-layouts  2.65 us (2%)
  between operations  2.38 us (2%)
    pallas_call x1, Pallas kernels, local_prog(): pl.pallas_call(functools.partial(kernel, dims), out_shape=(jax.ShapeDtype...  141 us

profile of v3, /device:TPU:1, one launch (start us, length us, event | category | flops | bytes accessed | tf_op | source)
XLA Modules:
  0.0 146.3 jit_solution(3227212157589446306)
XLA Ops:
  0.6 141.2 %lightgcn.1 = (bf16[64,256]{1,0:T(8,128)(2,1)}, bf16[16,64]{1,0:T(8,128)(2,1)}, f32[1,1]{1,0:T(1,128)}) custom-call(s32[32,256,128]{2,1,0:T(8,128)} %bitcast.5, bf16[64,256]{1,0:T(8,128)(2,1)} %bitcast.6, bf16[16,64]{1,0:T(8,128)(2,1)} %ei0.1, s32[3,128]{1,0:T(4,128)} %bitcast.8), custom_call_target="tpu_custom_call" | custom-call | tf_op jit(solution)/shard_map/lightgcn/pallas_call | solution.py:414
  141.9 1.4 copy.10
  143.3 1.3 copy.11

commit v4 on v3

--- a/solution.py
+++ b/solution.py
@@ -32,9 +32,11 @@
     (deg_s, deg_r, deg_f, own_deg, ideg, send_a, slab, slab_t, tbl0, tbl1, acc, ed0, ed1, ed2, pk_a, pk_b, pk_z, pk_q, pk_d, xc, xr,
      sends, recvs, a2a_recv, mask, load_sem) = scratch[:26]
     groups = (Z, G2, G2)
-    rs = [scratch[26 + 6 * n:32 + 6 * n] for n in range(3)]
+    p_1, rd_1, s1_1, rx_1, sy_1, ry_1, s2_1, rz_1, one_send, one_d, one_x, one_yz = scratch[26:38]
+    rs = [None] + [scratch[32 + 6 * n:38 + 6 * n] for n in (1, 2)]
     base = [SCATTER1]
-    for n in range(3):
+    base.append(SCATTER1)
+    for n in (1, 2):
         base.append(base[-1] + 2 * groups[n] + 1)
     row = lax.axis_index("row")
     col = lax.axis_index("col")
@@ -240,6 +242,63 @@
         await_send(s1.at[:, pl.ds(0, Q - 1)], base[n] + 1)
         await_send(s2.at[pl.ds(0, Z - 1)], base[n] + 2)
 
+    def remote1(src, dst, k, r, c, recv):
+        return pltpu.make_async_remote_copy(
+            src_ref=src, dst_ref=dst, send_sem=one_send.at[k], recv_sem=recv, device_id=(c, r), device_id_type=MESH)
+
+    def await1(ref, recv):
+        remote1(ref, ref, 0, row, col, recv).wait_recv()
+
+    def first_a(g):
+        def block(cy):
+            val = jnp.dot(slab_t[g * Y + cy], ed0[...], preferred_element_type=F32)
+            for i in range(R):
+                p_1[i % 2, g, i // 2, cy] = jnp.where(lane_left, val[i * SH:i * SH + HS], val[i * SH + HS:(i + 1) * SH])
+
+        lax.fori_loop(0, Y, lambda k, t: (block(k), t)[1], 0, unroll=4)
+        remote1(p_1.at[1 - core, g], rd_1.at[g], 0, mate, col, one_d.at[g]).start()
+
+    def first_b(g):
+        await1(rd_1.at[g], one_d.at[g])
+        for k in range(1, X):
+            to = (x + k) % X
+            s1_1[g, to] = p_1[core, g, to] + rd_1[g, to]
+        rx_1[g, x] = p_1[core, g, x] + rd_1[g, x]
+        for k in range(1, X):
+            to = (x + k) % X
+            remote1(s1_1.at[g, to], rx_1.at[g, x], 1, to * 2 + core, col, one_x.at[g]).start()
+
+    def first_c(g):
+        await1(rx_1.at[g, pl.ds(0, X - 1)], one_x.at[g])
+        total = rx_1[g, 0]
+        for k in range(1, X):
+            total = total + rx_1[g, k]
+        for cy in range(Y):
+            sy_1[cy, g] = total[cy]
+
+    def first_y():
+        for k in range(1, Y):
+            to = (y + k) % Y
+            remote1(sy_1.at[to], ry_1.at[y], 2, row, z * Y + to, one_yz.at[0]).start()
+        ry_1[y] = sy_1[y]
+
+    def first_z():
+        await1(ry_1.at[pl.ds(0, Y - 1)], one_yz.at[0])
+        total = ry_1[0]
+        for k in range(1, Y):
+            total = total + ry_1[k]
+        s2_1[...] = total
+        rz_1[z] = s2_1[z]
+        each(1, Z, lambda k: remote1(s2_1.at[(z + k) % Z], rz_1.at[z], 3, row, ((z + k) % Z) * Y + y, one_yz.at[1]).start())
+
+    def first_end():
+        await1(rz_1.at[pl.ds(0, Z - 1)], one_yz.at[1])
+        return lax.fori_loop(1, Z, lambda k, t: t + rz_1[k], rz_1[0], unroll=True).astype(BF16)
+
+    def first_sent():
+        for k, ref in enumerate((p_1.at[0], s1_1.at[:, pl.ds(0, X - 1)], sy_1.at[pl.ds(0, Y - 1)], s2_1.at[pl.ds(0, Z - 1)])):
+            remote1(ref, ref, k, row, col, one_yz.at[0]).wait_send()
+
     def source(k):
         dz, dy = order(k)
         return ((z - dz + Z) % Z) * Y + (y - dy + Y) % Y
@@ -263,15 +322,15 @@
 
     def stream(j):
         each(j * Y, (j + 1) * Y, arrive)
-        scatter_a(0, group(j), ed0)
+        first_a(group(j))
 
         @pl.when(j >= 1)
         def _():
-            scatter_b(0, group(j - 1))
+            first_b(group(j - 1))
 
         @pl.when(j >= 2)
         def _():
-            scatter_c(0, group(j - 2))
+            first_c(group(j - 2))
 
     each(0, Z - 1, stream)
     each((Z - 1) * Y, C - 1, arrive)
@@ -280,24 +339,28 @@
     def twice(v):
         return jnp.where(wide_left, v, swap(v)).astype(BF16)
 
+    first_a(z)
+    first_b(group(Z - 2))
     user1 = acc[...].astype(BF16).astype(F32)
     ed1[...] = twice(user1)
     for g in range(G2):
         scatter_a(1, g, ed1)
-        if g > 0:
+        if g == 0:
+            first_b(z)
+        else:
             scatter_b(1, g - 1)
-    scatter_a(0, z, ed0)
     scatter_b(1, G2 - 1)
-    scatter_b(0, group(Z - 2))
-    scatter_b(0, z)
     if Z > 2:
-        scatter_c(0, group(Z - 3))
-    scatter_c(1, 0)
-    scatter_c(0, group(Z - 2))
-    scatter_c(0, z)
-    for g in range(1, G2):
+        first_c(group(Z - 3))
+    first_c(group(Z - 2))
+    first_c(z)
+    first_y()
+    for g in range(G2 // 2):
         scatter_c(1, g)
-    item1 = scatter_end(0).astype(F32)
+    first_z()
+    for g in range(G2 // 2, G2):
+        scatter_c(1, g)
+    item1 = first_end().astype(F32)
     item2 = scatter_end(1).astype(F32)
     low = jnp.where(lane_left, item1, swap(item2))
     high = jnp.where(lane_left, swap(item1), item2)
@@ -379,7 +442,8 @@
     await_send(send_a.at[pl.ds(0, C - 1)], ATOA)
     gather_sent(tbl0, GATHER0)
     gather_sent(tbl1, GATHER1)
-    for n in range(3):
+    first_sent()
+    for n in (1, 2):
         scatter_sent(n)
     await_send(pk_b, PICK)
     await_send(pk_z.at[pl.ds(0, Z - 1)], PICK + 1)
@@ -403,10 +467,15 @@
         vm((Z, PICKS, WIDE), BF16), vm((Q, PICKS, WIDE), BF16), vm((2, PICKS, WIDE), BF16),
         vm((C, 1, TRIPLES), F32), vm((R, 1, TRIPLES), F32),
     ]
-    count = SCATTER1 + sum(2 * g + 1 for g in (Z, G2, G2)) + 1
-    scratch += [pltpu.SemaphoreType.DMA((count,)), pltpu.SemaphoreType.DMA((count,)), pltpu.SemaphoreType.DMA((C,)),
-                vm((C, UD, IB), jnp.int32), pltpu.SemaphoreType.DMA((LOADS,))]
-    for g in (Z, G2, G2):
+    count = SCATTER1 + 2 * (2 * G2 + 1)
+    sem = pltpu.SemaphoreType.DMA
+    scratch += [sem((count,)), sem((count,)), sem((C,)), vm((C, UD, IB), jnp.int32), sem((LOADS,))]
+    scratch += [
+        vm((2, Z, X, Y, HS, WIDE), F32), vm((Z, X, Y, HS, WIDE), F32), vm((Z, X, Y, HS, WIDE), F32), vm((Z, X, Y, HS, WIDE), F32),
+        vm((Y, Z, HS, WIDE), F32), vm((Y, Z, HS, WIDE), F32), vm((Z, HS, WIDE), F32), vm((Z, HS, WIDE), F32),
+        sem((4,)), sem((Z,)), sem((Z,)), sem((2,)),
+    ]
+    for g in (G2, G2):
         scratch += [vm((2, g, Q, Z // g, HS, WIDE), F32)] + [vm((g, Q, Z // g, HS, WIDE), F32)] * 3 + [vm((Z, HS, WIDE), F32)] * 2
     dims = (Z, Y, X, SH, UD, G2)
 

time: 147 us -> 141 us (0.959)
  Pallas kernels: 141 us -> 136 us
    pallas_call x1, Pallas kernels: 141 us -> 136 us  [local_prog(): pl.pallas_call(functools.partial(kernel, dims), out_shape=(jax.ShapeDtype...]
where the time goes in v4:
time: 141 us
  Pallas kernels  136 us (96%)
  local copies, waits for them, and re-layouts  2.65 us (2%)
  between operations  2.38 us (2%)
    pallas_call x1, Pallas kernels, local_prog(): pl.pallas_call(functools.partial(kernel, dims), out_shape=(jax.ShapeDtype...  136 us

profile of v4, /device:TPU:1, one launch (start us, length us, event | category | flops | bytes accessed | tf_op | source)
XLA Modules:
  0.0 140.8 jit_solution(4802526089144553325)
XLA Ops:
  0.6 135.8 %lightgcn.1 = (bf16[64,256]{1,0:T(8,128)(2,1)}, bf16[16,64]{1,0:T(8,128)(2,1)}, f32[1,1]{1,0:T(1,128)}) custom-call(s32[32,256,128]{2,1,0:T(8,128)} %bitcast.5, bf16[64,256]{1,0:T(8,128)(2,1)} %bitcast.6, bf16[16,64]{1,0:T(8,128)(2,1)} %ei0.1, s32[3,128]{1,0:T(4,128)} %bitcast.8), custom_call_target="tpu_custom_call" | custom-call | tf_op jit(solution)/shard_map/lightgcn/pallas_call | solution.py:483
  136.4 1.4 copy.10
  137.8 1.3 copy.11

commit v5 on v4

--- a/solution.py
+++ b/solution.py
@@ -31,6 +31,7 @@
     HS = SH // 2
     (deg_s, deg_r, deg_f, own_deg, ideg, send_a, slab, slab_t, tbl0, tbl1, acc, ed0, ed1, ed2, pk_a, pk_b, pk_z, pk_q, pk_d, xc, xr,
      sends, recvs, a2a_recv, mask, load_sem) = scratch[:26]
+    spread_recv = scratch[50]
     groups = (Z, G2, G2)
     p_1, rd_1, s1_1, rx_1, sy_1, ry_1, s2_1, rz_1, one_send, one_d, one_x, one_yz = scratch[26:38]
     rs = [None] + [scratch[32 + 6 * n:38 + 6 * n] for n in (1, 2)]
@@ -134,46 +135,50 @@
             parts += [v, swap(v)]
         return jnp.concatenate(parts, axis=0).astype(BF16)
 
+    def order(k):
+        j = k // Y
+        m = (j + 1) // 2
+        odd = j % 2
+        return (odd * m + (1 - odd) * (Z - m)) % Z, k % Y
+
+    def target(k):
+        dz, dy = order(k)
+        return ((z + dz) % Z) * Y + (y + dy) % Y
+
     each(1, C, lambda k: remote(deg_s.at[(col + k) % C], deg_r.at[col], DEG, row, (col + k) % C).start())
     each(1, R, lambda k: remote(ideg.at[row], ideg.at[row], IDEG, (row + k) % R, col).start())
     gather_z(tbl0, GATHER0)
     await_recv(deg_r.at[pl.ds(0, C - 1)], DEG)
     own_deg[...] = lax.fori_loop(0, C, lambda k, t: t + deg_r[k], jnp.zeros((1, UD), F32), unroll=True)
     deg_f[col] = own_deg[...]
-    each(1, C, lambda k: remote(own_deg, deg_f.at[col], SPREAD, row, (col + k) % C).start())
+    each(1, C, lambda k: remote(own_deg, deg_f.at[col], SPREAD, row, target(k), recv=spread_recv.at[col]).start())
     await_recv(ideg.at[pl.ds(0, R - 1)], IDEG)
     scale_item = lax.rsqrt(jnp.maximum(lax.fori_loop(0, R, lambda k, t: t + ideg[k], jnp.zeros((1, IB), F32), unroll=True), 1.0))
     gather_q(tbl0, GATHER0)
-    await_recv(deg_f.at[pl.ds(0, C - 1)], SPREAD)
-
-    def order(k):
-        j, dy = k // Y, (k + 1) % Y
-        m = Z // 2 - (j + 1) // 2
-        odd = j % 2
-        return (odd * m + (1 - odd) * (Z - m)) % Z, dy
 
     def piece(c):
         scale = lax.rsqrt(jnp.maximum(deg_f[c], 1.0))
         scale = jnp.transpose(jnp.broadcast_to(scale, (IB, UD)))
         return (mask[c].astype(F32) * scale * scale_item).astype(BF16)
 
-    def target(k):
-        dz, dy = order(k)
-        return ((z + dz) % Z) * Y + (y + dy) % Y
-
     def ship(k):
         to = target(k)
         remote(send_a.at[to], slab.at[col], ATOA, row, to, recv=a2a_recv.at[col]).start()
 
-    send_a[target(0)] = piece(target(0))
+    def make(k):
+        to = target(k)
+        remote(deg_f.at[to], deg_f.at[to], SPREAD, row, col, recv=spread_recv.at[to]).wait_recv()
+        send_a[to] = piece(to)
+
+    make(1)
 
     def make_and_ship(k):
-        send_a[target(k)] = piece(target(k))
+        make(k)
         ship(k - 1)
 
-    each(1, C - 1, make_and_ship)
+    each(2, C, make_and_ship)
     slab[col] = piece(col)
-    ship(C - 2)
+    ship(C - 1)
     gather_d(tbl0, GATHER0)
     gather_end(tbl0, GATHER0)
 
@@ -319,41 +324,35 @@
 
     acc[...] = jnp.zeros_like(acc)
     use(col)
+    each(1, Y, arrive)
+    first_a(z)
 
     def stream(j):
         each(j * Y, (j + 1) * Y, arrive)
         first_a(group(j))
-
-        @pl.when(j >= 1)
-        def _():
-            first_b(group(j - 1))
+        first_b(group(j - 1))
 
         @pl.when(j >= 2)
         def _():
             first_c(group(j - 2))
 
-    each(0, Z - 1, stream)
-    each((Z - 1) * Y, C - 1, arrive)
+    each(1, Z, stream)
     wide_left = lax.broadcasted_iota(jnp.int32, (UD, WIDE), 1) < FEAT
 
     def twice(v):
         return jnp.where(wide_left, v, swap(v)).astype(BF16)
 
-    first_a(z)
-    first_b(group(Z - 2))
     user1 = acc[...].astype(BF16).astype(F32)
     ed1[...] = twice(user1)
     for g in range(G2):
         scatter_a(1, g, ed1)
         if g == 0:
-            first_b(z)
+            first_b(group(Z - 1))
         else:
             scatter_b(1, g - 1)
     scatter_b(1, G2 - 1)
-    if Z > 2:
-        first_c(group(Z - 3))
     first_c(group(Z - 2))
-    first_c(z)
+    first_c(group(Z - 1))
     first_y()
     for g in range(G2 // 2):
         scatter_c(1, g)
@@ -477,6 +476,7 @@
     ]
     for g in (G2, G2):
         scratch += [vm((2, g, Q, Z // g, HS, WIDE), F32)] + [vm((g, Q, Z // g, HS, WIDE), F32)] * 3 + [vm((Z, HS, WIDE), F32)] * 2
+    scratch += [sem((C,))]
     dims = (Z, Y, X, SH, UD, G2)
 
     def local_prog(mask_blk, user_shard, item_shard, triples):

time: 141 us -> 141 us (level)
  no operation moved by 1% of the time
where the time goes in v5:
time: 141 us; the launch traced here: 140 us
  Pallas kernels  135 us (96%)
  local copies, waits for them, and re-layouts  2.65 us (2%)
  between operations  2.38 us (2%)
    pallas_call x1, Pallas kernels, local_prog(): pl.pallas_call(functools.partial(kernel, dims), out_shape=(jax.ShapeDtype...  135 us

profile of v5, /device:TPU:1, one launch (start us, length us, event | category | flops | bytes accessed | tf_op | source)
XLA Modules:
  0.0 140.5 jit_solution(10883401486836883839)
XLA Ops:
  0.6 135.4 %lightgcn.1 = (bf16[64,256]{1,0:T(8,128)(2,1)}, bf16[16,64]{1,0:T(8,128)(2,1)}, f32[1,1]{1,0:T(1,128)}) custom-call(s32[32,256,128]{2,1,0:T(8,128)} %bitcast.5, bf16[64,256]{1,0:T(8,128)(2,1)} %bitcast.6, bf16[16,64]{1,0:T(8,128)(2,1)} %ei0.1, s32[3,128]{1,0:T(4,128)} %bitcast.8), custom_call_target="tpu_custom_call" | custom-call | tf_op jit(solution)/shard_map/lightgcn/pallas_call | solution.py:483
  136.1 1.4 copy.10
  137.5 1.3 copy.11

commit v6 on v5

--- a/solution.py
+++ b/solution.py
@@ -78,8 +78,13 @@
         pl.semaphore_signal(barrier, inc=1, device_id=(c, r), device_id_type=MESH)
 
     each(1, C, lambda k: hail((col + k) % C, row))
+    each(1, Y, lambda k: hail(z * Y + (y + k) % Y, mate))
     each(1, R, lambda k: hail(col, (row + k) % R))
-    each(0, (X - 1) * (Y - 1), lambda k: hail(z * Y + (y + 1 + k // (X - 1)) % Y, ((x + 1 + k % (X - 1)) % X) * 2 + core))
+    def hail_diagonal(k):
+        i = k // 2
+        hail(z * Y + (y + 1 + i // (X - 1)) % Y, ((x + 1 + i % (X - 1)) % X) * 2 + k % 2)
+
+    each(0, 2 * (X - 1) * (Y - 1), hail_diagonal)
 
     ones = jnp.ones((8, IB), BF16)
 
@@ -106,7 +111,7 @@
     tbl0[core, q, z] = item0.astype(BF16)
     user0 = eu0[...].astype(F32)
     ed0[...] = jnp.transpose(jnp.concatenate([user0, user0], axis=0)).astype(BF16)
-    pl.semaphore_wait(barrier, (C - 1) + (R - 1) + (X - 1) * (Y - 1))
+    pl.semaphore_wait(barrier, (C - 1) + (Y - 1) + (R - 1) + 2 * (X - 1) * (Y - 1))
 
     def gather_z(tbl, sem):
         each(1, Z, lambda k: remote(tbl.at[core, q, z], tbl.at[core, q, z], sem, row, ((z + k) % Z) * Y + y).start())
@@ -425,13 +430,19 @@
     own = lax.broadcasted_iota(jnp.int32, (SH, TRIPLES), 0) + (col * R + row) * SH
     pos = jnp.sum(jnp.where(own == trip[1:2, :], dots, 0.0), axis=0, keepdims=True)
     neg = jnp.sum(jnp.where(own == trip[2:3, :], dots, 0.0), axis=0, keepdims=True)
-    xc[col] = pos - neg
-    each(1, C, lambda k: remote(xc.at[col], xc.at[col], MARGIN, row, (col + k) % C).start())
-    await_recv(xc.at[pl.ds(0, C - 1)], MARGIN)
-    xr[row] = lax.fori_loop(1, C, lambda k, t: t + xc[k], xc[0], unroll=True)
-    each(1, R, lambda k: remote(xr.at[row], xr.at[row], MARGIN + 1, (row + k) % R, col).start())
-    await_recv(xr.at[pl.ds(0, R - 1)], MARGIN + 1)
-    margin = lax.fori_loop(1, R, lambda k, t: t + xr[k], xr[0], unroll=True)
+    mine = q * 2 + core
+    xc[mine] = pos - neg
+
+    def spread_margin(k):
+        to = (mine + k) % (2 * Q)
+        remote(xc.at[mine], xc.at[mine], MARGIN, ((to // 2) % X) * 2 + to % 2, z * Y + to // (2 * X)).start()
+
+    each(1, 2 * Q, spread_margin)
+    await_recv(xc.at[pl.ds(0, 2 * Q - 1)], MARGIN)
+    xr[z] = lax.fori_loop(1, 2 * Q, lambda k, t: t + xc[k], xc[0], unroll=True)
+    each(1, Z, lambda k: remote(xr.at[z], xr.at[z], MARGIN + 1, row, ((z + k) % Z) * Y + y).start())
+    await_recv(xr.at[pl.ds(0, Z - 1)], MARGIN + 1)
+    margin = lax.fori_loop(1, Z, lambda k, t: t + xr[k], xr[0], unroll=True)
     soft = jnp.maximum(-margin, 0.0) + jnp.log1p(jnp.exp(-jnp.abs(margin)))
     loss[...] = jnp.sum(soft, axis=1, keepdims=True) / TRIPLES
 
@@ -448,8 +459,14 @@
     await_send(pk_z.at[pl.ds(0, Z - 1)], PICK + 1)
     await_send(pk_q.at[pl.ds(0, Q - 1)], PICK + 2)
     await_send(pk_d.at[0], PICK + 3)
-    await_send(xc.at[pl.ds(0, C - 1)], MARGIN)
-    await_send(xr.at[pl.ds(0, R - 1)], MARGIN + 1)
+    await_send(xc.at[pl.ds(0, 2 * Q - 1)], MARGIN)
+    await_send(xr.at[pl.ds(0, Z - 1)], MARGIN + 1)
+
+
+def emit(user_in, item_in, loss_in, user_out, item_out, loss_out):
+    user_out[...] = user_in[...]
+    item_out[...] = item_in[...]
+    loss_out[...] = loss_in[...]
 
 
 def build(mesh, Y, SH, UD, G2):
@@ -464,7 +481,7 @@
         vm((UD, WIDE), F32), vm((UD, WIDE), BF16), vm((UD, WIDE), BF16), vm((UD, WIDE), BF16),
         vm((2, PICKS, WIDE), BF16), vm((PICKS, WIDE), BF16),
         vm((Z, PICKS, WIDE), BF16), vm((Q, PICKS, WIDE), BF16), vm((2, PICKS, WIDE), BF16),
-        vm((C, 1, TRIPLES), F32), vm((R, 1, TRIPLES), F32),
+        vm((2 * Q, 1, TRIPLES), F32), vm((Z, 1, TRIPLES), F32),
     ]
     count = SCATTER1 + 2 * (2 * G2 + 1)
     sem = pltpu.SemaphoreType.DMA
@@ -494,6 +511,17 @@
                 collective_id=0, has_side_effects=True, vmem_limit_bytes=60 * 1024 * 1024),
             name="lightgcn",
         )(mask_blk.reshape(C, UD, IB), user_shard.T, item_shard, triples.T)
+        out_user, out_item, loss = pl.pallas_call(
+            emit,
+            out_shape=(
+                jax.ShapeDtypeStruct((FEAT, UD), BF16),
+                jax.ShapeDtypeStruct((SH, FEAT), BF16),
+                jax.ShapeDtypeStruct((1, 1), F32),
+            ),
+            in_specs=[pl.BlockSpec(memory_space=pltpu.VMEM)] * 3,
+            out_specs=(pl.BlockSpec(memory_space=pltpu.VMEM),) * 3,
+            name="emit",
+        )(out_user, out_item, loss)
         return out_user.T, out_item, loss[0, 0]
 
     return jax.shard_map(

time: 141 us -> 138 us (0.979)
  local copies, waits for them, and re-layouts: 2.65 us -> 0 us
  Pallas kernels: 135 us -> 137 us
  between operations: 2.38 us -> 0.64 us
    unnamed x2 -> x0, local copies, waits for them, and re-layouts: 2.65 us -> none
    pallas_call x0 -> x1, Pallas kernels: none -> 2 us  [local_prog(): pl.pallas_call(emit, out_shape=(jax.ShapeDtypeStruct((FEAT, UD), BF16), j...]
where the time goes in v6:
time: 138 us
  Pallas kernels  137 us (99%)
    pallas_call x1, Pallas kernels, local_prog(): pl.pallas_call(functools.partial(kernel, dims), out_shape=(jax.ShapeDtype...  135 us

profile of v6, /device:TPU:1, one launch (start us, length us, event | category | flops | bytes accessed | tf_op | source)
XLA Modules:
  0.0 138.1 jit_solution(14673011764987764593)
XLA Ops:
  0.6 135.4 %lightgcn.1 = (bf16[64,256]{1,0:T(8,128)(2,1)}, bf16[16,64]{1,0:T(8,128)(2,1)}, f32[1,1]{1,0:T(1,128)}) custom-call(s32[32,256,128]{2,1,0:T(8,128)} %bitcast.5, bf16[64,256]{1,0:T(8,128)(2,1)} %bitcast.6, bf16[16,64]{1,0:T(8,128)(2,1)} %ei0.1, s32[3,128]{1,0:T(4,128)} %bitcast.7), custom_call_target="tpu_custom_call" | custom-call | tf_op jit(solution)/shard_map/lightgcn/pallas_call | solution.py:500
  136.1 2.0 %emit.1 = (bf16[64,256]{1,0:T(8,128)(2,1)}, bf16[16,64]{1,0:T(8,128)(2,1)}, f32[1,1]{1,0:T(1,128)}) custom-call(bf16[64,256]{1,0:T(8,128)(2,1)} %get-tuple-element.9.user_in, bf16[16,64]{1,0:T(8,128)(2,1)} %get-tuple-element.10.item_in, f32[1,1]{1,0:T(1,128)} %get-tuple-element.11.loss_in), custom_call_target="tpu_custom_call" | custom-call | tf_op jit(solution)/shard_map/emit/pallas_call | solution.py:514

commit v7 on v6

--- a/solution.py
+++ b/solution.py
@@ -531,4 +531,4 @@
 
 
 def solution(mesh):
-    return build(mesh, Y=4, SH=16, UD=256, G2=4)
+    return build(mesh, Y=4, SH=16, UD=256, G2=8)

time: 138 us -> 138 us (level)
  no operation moved by 1% of the time
where the time goes in v7:
time: 138 us
  Pallas kernels  137 us (99%)
    pallas_call x1, Pallas kernels, local_prog(): pl.pallas_call(functools.partial(kernel, dims), out_shape=(jax.ShapeDtype...  135 us

profile of v7, /device:TPU:1, one launch (start us, length us, event | category | flops | bytes accessed | tf_op | source)
XLA Modules:
  0.0 137.8 jit_solution(1976325292559867520)
XLA Ops:
  0.6 135.2 %lightgcn.1 = (bf16[64,256]{1,0:T(8,128)(2,1)}, bf16[16,64]{1,0:T(8,128)(2,1)}, f32[1,1]{1,0:T(1,128)}) custom-call(s32[32,256,128]{2,1,0:T(8,128)} %bitcast.5, bf16[64,256]{1,0:T(8,128)(2,1)} %bitcast.6, bf16[16,64]{1,0:T(8,128)(2,1)} %ei0.1, s32[3,128]{1,0:T(4,128)} %bitcast.7), custom_call_target="tpu_custom_call" | custom-call | tf_op jit(solution)/shard_map/lightgcn/pallas_call | solution.py:500
  135.8 2.0 %emit.1 = (bf16[64,256]{1,0:T(8,128)(2,1)}, bf16[16,64]{1,0:T(8,128)(2,1)}, f32[1,1]{1,0:T(1,128)}) custom-call(bf16[64,256]{1,0:T(8,128)(2,1)} %get-tuple-element.9.user_in, bf16[16,64]{1,0:T(8,128)(2,1)} %get-tuple-element.10.item_in, f32[1,1]{1,0:T(1,128)} %get-tuple-element.11.loss_in), custom_call_target="tpu_custom_call" | custom-call | tf_op jit(solution)/shard_map/emit/pallas_call | solution.py:514

commit v8 on v7

--- a/solution.py
+++ b/solution.py
@@ -355,14 +355,12 @@
             first_b(group(Z - 1))
         else:
             scatter_b(1, g - 1)
-    scatter_b(1, G2 - 1)
     first_c(group(Z - 2))
     first_c(group(Z - 1))
     first_y()
-    for g in range(G2 // 2):
-        scatter_c(1, g)
+    scatter_b(1, G2 - 1)
     first_z()
-    for g in range(G2 // 2, G2):
+    for g in range(G2):
         scatter_c(1, g)
     item1 = first_end().astype(F32)
     item2 = scatter_end(1).astype(F32)

time: 138 us -> 138 us (level)
  no operation moved by 1% of the time
where the time goes in v8:
time: 138 us
  Pallas kernels  137 us (99%)
    pallas_call x1, Pallas kernels, local_prog(): pl.pallas_call(functools.partial(kernel, dims), out_shape=(jax.ShapeDtype...  135 us

profile of v8, /device:TPU:1, one launch (start us, length us, event | category | flops | bytes accessed | tf_op | source)
XLA Modules:
  0.0 137.8 jit_solution(13387961368636167449)
XLA Ops:
  0.6 135.1 %lightgcn.1 = (bf16[64,256]{1,0:T(8,128)(2,1)}, bf16[16,64]{1,0:T(8,128)(2,1)}, f32[1,1]{1,0:T(1,128)}) custom-call(s32[32,256,128]{2,1,0:T(8,128)} %bitcast.5, bf16[64,256]{1,0:T(8,128)(2,1)} %bitcast.6, bf16[16,64]{1,0:T(8,128)(2,1)} %ei0.1, s32[3,128]{1,0:T(4,128)} %bitcast.7), custom_call_target="tpu_custom_call" | custom-call | tf_op jit(solution)/shard_map/lightgcn/pallas_call | solution.py:498
  135.8 2.0 %emit.1 = (bf16[64,256]{1,0:T(8,128)(2,1)}, bf16[16,64]{1,0:T(8,128)(2,1)}, f32[1,1]{1,0:T(1,128)}) custom-call(bf16[64,256]{1,0:T(8,128)(2,1)} %get-tuple-element.9.user_in, bf16[16,64]{1,0:T(8,128)(2,1)} %get-tuple-element.10.item_in, f32[1,1]{1,0:T(1,128)} %get-tuple-element.11.loss_in), custom_call_target="tpu_custom_call" | custom-call | tf_op jit(solution)/shard_map/emit/pallas_call | solution.py:512

commit v9 on v8

--- a/solution.py
+++ b/solution.py
@@ -381,7 +381,6 @@
     lax.fori_loop(0, C, lambda k, t: (absorb(k), t)[1], 0, unroll=4)
     late = acc[...].astype(BF16).astype(F32)
     ed2[...] = twice(late)
-    scatter_a(2, 0, ed2)
     sum_user = ((ed0[...].astype(F32) + ed1[...].astype(F32)) + ed2[...].astype(F32)) + jnp.where(wide_left, swap(late), late)
     user_rows = (sum_user / (LAYERS + 1)).astype(BF16)
 
@@ -393,6 +392,7 @@
         lo, hi = h * PICKS, (h + 2) * PICKS
         pk_a[h] = jnp.where(pick_left, found[lo:lo + PICKS], found[hi:hi + PICKS]).astype(BF16)
     remote(pk_a.at[1 - core], pk_b, PICK, mate, col).start()
+    scatter_a(2, 0, ed2)
     for g in range(1, G2):
         scatter_a(2, g, ed2)
         if g == 1:

time: 138 us -> 138 us (level)
  no operation moved by 1% of the time
where the time goes in v9:
time: 138 us
  Pallas kernels  137 us (99%)
    pallas_call x1, Pallas kernels, local_prog(): pl.pallas_call(functools.partial(kernel, dims), out_shape=(jax.ShapeDtype...  135 us

profile of v9, /device:TPU:1, one launch (start us, length us, event | category | flops | bytes accessed | tf_op | source)
XLA Modules:
  0.0 137.7 jit_solution(18247110868564591336)
XLA Ops:
  0.6 135.1 %lightgcn.1 = (bf16[64,256]{1,0:T(8,128)(2,1)}, bf16[16,64]{1,0:T(8,128)(2,1)}, f32[1,1]{1,0:T(1,128)}) custom-call(s32[32,256,128]{2,1,0:T(8,128)} %bitcast.5, bf16[64,256]{1,0:T(8,128)(2,1)} %bitcast.6, bf16[16,64]{1,0:T(8,128)(2,1)} %ei0.1, s32[3,128]{1,0:T(4,128)} %bitcast.7), custom_call_target="tpu_custom_call" | custom-call | tf_op jit(solution)/shard_map/lightgcn/pallas_call | solution.py:498
  135.7 2.0 %emit.1 = (bf16[64,256]{1,0:T(8,128)(2,1)}, bf16[16,64]{1,0:T(8,128)(2,1)}, f32[1,1]{1,0:T(1,128)}) custom-call(bf16[64,256]{1,0:T(8,128)(2,1)} %get-tuple-element.9.user_in, bf16[16,64]{1,0:T(8,128)(2,1)} %get-tuple-element.10.item_in, f32[1,1]{1,0:T(1,128)} %get-tuple-element.11.loss_in), custom_call_target="tpu_custom_call" | custom-call | tf_op jit(solution)/shard_map/emit/pallas_call | solution.py:512
